TPU v7x, 128 devices: a whole 4x4x4 slice. The times are simulated.
128 devices in a mesh: patch: 64 (over y, x_hi, z, core), band: 2 (over x_lo).
Axes of the slice: x: 4 (x_hi: 2, x_lo: 2; x = x_hi * 2 + x_lo), y: 4, z: 4, core: 2. Of those that a mesh axis runs over, the one named last changes fastest.
Arguments:
- latents: float32 [40960, 512], P('patch', 'band'), may hold values from -6 to 6
- edge_latents: float32 [327680, 512], P(('patch', 'band')), may hold values from -6 to 6
- edge_sender: int32 [327680], P(('patch', 'band')), may hold values from 0 to 1343, as said below
- edge_receiver: int32 [327680], P(('patch', 'band')), may hold values from 0 to 319
- block_counts: int32 [2560], P(('patch', 'band')), may hold values from 16 to 128, as said below
- send_rows: int32 [128, 128, 8], P(('patch', 'band')), may hold values from 0 to 319
- edge_first_weight: bfloat16 [2, 1536, 512], replicated, may hold values from -0.15625 to 0.15625
- edge_first_bias: float32 [2, 512], replicated, may hold values from -3 to 3
- edge_second_weight: bfloat16 [2, 512, 512], replicated
- edge_gain: float32 [2, 512], replicated, may hold values from 0.1 to 1.9
- edge_offset: float32 [2, 512], replicated, may hold values from -3 to 3
- node_first_weight: bfloat16 [2, 1024, 512], replicated, may hold values from -0.1875 to 0.1875
- node_first_bias: float32 [2, 512], replicated, may hold values from -3 to 3
- node_second_weight: bfloat16 [2, 512, 512], replicated
- node_gain: float32 [2, 512], replicated, may hold values from 0.1 to 1.9
- node_offset: float32 [2, 512], replicated, may hold values from -3 to 3
Outputs:
- new_nodes: float32 [40960, 512], P(('patch', 'band'))
- new_edges: float32 [327680, 512], P(('patch', 'band'))
Inputs may be any that keep to these rules, and one draw needn't show every extreme that they name: `edge_sender`: an entry below 320 names a node row of the edge's own device; an entry k above names slot (k - 320) % 8 of the rows that device (k - 320) // 8 sends to the edge's device. `block_counts`: the used slots of a block are its first ones; every device has a full block. send_rows[d, q] lists node rows of device d, numbered within d, that device q receives from d.
All inputs are finite; a program needn't handle non-finite values.
Results may differ from a plain program's by a relative error of at most 0.0045.
Values may be sent and summed in bfloat16 or wider, within the bound.
A program may use at most 128 MiB of HBM per device.

v0:
```python
import jax
import jax.numpy as jnp
from jax import lax
from jax.sharding import PartitionSpec as P

epsilon = 1e-05


def layer_norm(values, norm_gain, norm_offset):
    centre = values - jnp.mean(values, axis=-1, keepdims=True)
    spread = jnp.mean(centre * centre, axis=-1, keepdims=True)
    return centre * lax.rsqrt(spread + epsilon) * norm_gain + norm_offset


def perceptron(pieces, first_weight, first_bias, second_weight, norm_gain, norm_offset):
    columns = pieces[0].shape[1]
    running = first_bias
    for position in range(len(pieces)):
        running = running + jnp.dot(
            pieces[position],
            first_weight[position * columns : (position + 1) * columns],
            preferred_element_type=jnp.float32,
        )
    active = (running * jax.nn.sigmoid(running)).astype(jnp.bfloat16)
    result = jnp.dot(active, second_weight, preferred_element_type=jnp.float32)
    return layer_norm(result, norm_gain, norm_offset)


def fetch_halo(node_low, send_lists):
    outgoing = node_low[send_lists]
    return lax.all_to_all(outgoing, ("patch", "band"), split_axis=0, concat_axis=0, tiled=True)


def shards(
    latents,
    edge_latents,
    edge_sender,
    edge_receiver,
    block_counts,
    send_rows,
    edge_first_weight,
    edge_first_bias,
    edge_second_weight,
    edge_gain,
    edge_offset,
    node_first_weight,
    node_first_bias,
    node_second_weight,
    node_gain,
    node_offset,
):
    layers = edge_first_weight.shape[0]
    send_lists = send_rows[0]
    block_length = edge_sender.shape[0] // block_counts.shape[0]
    usable = (jnp.arange(block_length, dtype=jnp.int32)[None, :] < block_counts[:, None]).reshape(
        -1
    )
    first_rows = None
    node_state = lax.all_to_all(latents, "band", split_axis=0, concat_axis=1, tiled=True)
    edge_state = edge_latents
    node_count = node_state.shape[0]
    matches = jnp.arange(node_count, dtype=jnp.int32)[:, None] == edge_receiver[None, :]
    receiver_hot = matches.astype(jnp.bfloat16)
    summing_hot = (matches & usable[None, :]).astype(jnp.bfloat16)
    for layer_index in range(layers):
        node_low = node_state.astype(jnp.bfloat16)
        incoming = fetch_halo(node_low, send_lists)
        sender_table = jnp.concatenate([node_low, incoming.reshape(-1, node_low.shape[1])], axis=0)
        receiver_rows = lax.dot_general(
            receiver_hot, node_low, (((0,), (0,)), ((), ())), preferred_element_type=jnp.float32
        ).astype(jnp.bfloat16)
        edge_low = edge_state.astype(jnp.bfloat16)
        update = perceptron(
            (edge_low, sender_table[edge_sender], receiver_rows),
            edge_first_weight[layer_index],
            edge_first_bias[layer_index],
            edge_second_weight[layer_index],
            edge_gain[layer_index],
            edge_offset[layer_index],
        )
        edge_state = edge_state + jnp.where(usable[:, None], update, jnp.zeros_like(update))
        edge_out_low = edge_state.astype(jnp.bfloat16)
        summed = jnp.dot(summing_hot, edge_out_low, preferred_element_type=jnp.float32)
        summed_low = summed.astype(jnp.bfloat16)
        node_state = node_state + perceptron(
            (node_low, summed_low),
            node_first_weight[layer_index],
            node_first_bias[layer_index],
            node_second_weight[layer_index],
            node_gain[layer_index],
            node_offset[layer_index],
        )
    return (node_state, edge_state)


def solution(mesh):
    return jax.shard_map(
        shards,
        mesh=mesh,
        in_specs=(
            P("patch", "band"),
            P(("patch", "band"), None),
            P(("patch", "band")),
            P(("patch", "band")),
            P(("patch", "band")),
            P(("patch", "band"), None, None),
            P(),
            P(),
            P(),
            P(),
            P(),
            P(),
            P(),
            P(),
            P(),
            P(),
        ),
        out_specs=(P(("patch", "band"), None), P(("patch", "band"), None)),
        check_vma=False,
    )
```

profile of v0, /device:TPU:1, one launch (start us, length us, event | category | flops | bytes accessed | tf_op | source)
XLA Modules:
  0.0 172.8 jit_solution(914075629936271546)
XLA Ops:
  0.6 3.5 %all-to-all-start = ((f32[2,320,256]{2,1,0:T(8,128)}), f32[2,320,256]{2,1,0:T(8,128)S(1)}, u32[]{:S(2)}, u32[]{:S(2)}) async-start(f32[2,320,256]{2,1,0:T(8,128)} %bitcast.107), calls=%async_computation | async-start | bytes 1310720 | tf_op jit(solution)/shard_map/all_to_all | solution.py:59
  8.9 6.4 %fusion.6 = f32[2560,512]{1,0:T(8,128)} fusion(f32[2560,512]{1,0:T(8,128)} %param.17, bf16[2,1536,512]{2,1,0:T(8,128)(2,1)} %param.22), kind=kOutput, calls=%fused_computation.17 | convolution fusion | flops 1343488000 | bytes 11010048 | tf_op jit(solution)/shard_map/dot_general | solution.py:19
  15.6 5.1 %gather_fusion = bf16[1024,512]{1,0:T(8,128)(2,1)} fusion(bf16[320,512]{1,0:T(8,128)(2,1)S(1)} %convert_element_type.50, s32[1024]{0:T(1024)S(1)} %broadcast_clamp_fusion), kind=kCustom, calls=%fused_computation | custom fusion | bytes 2101248 | tf_op jit(solution)/shard_map/gather | solution.py:30
  20.7 12.5 %all-to-all-start.1 = ((bf16[128,8,512]{2,1,0:T(8,128)(2,1)}), bf16[128,8,512]{2,1,0:T(8,128)(2,1)}, u32[]{:S(2)}, u32[]{:S(2)}) async-start(bf16[128,8,512]{2,1,0:T(8,128)(2,1)} %bitcast.104), calls=%async_computation.1 | async-start | bytes 2097152 | tf_op jit(solution)/shard_map/all_to_all | solution.py:31
  33.2 5.9 %copy.32 = f32[2560,512]{0,1:T(8,128)} copy(f32[2560,512]{1,0:T(8,128)} %param.17) | data formatting | bytes 10485760 | tf_op args[1]
  39.2 2.2 %convolution_add_fusion.3 = f32[320,512]{1,0:T(8,128)} fusion(bf16[320,512]{1,0:T(8,128)(2,1)S(1)} %bitcast.106, bf16[2,1024,512]{2,1,0:T(8,128)(2,1)} %param.27, f32[512]{0:T(512)S(1)} %bitcast.115), kind=kOutput, calls=%fused_computation.35 | convolution fusion | flops 167936000 | bytes 1509376 | tf_op jit(solution)/shard_map/dot_general | solution.py:19
  41.4 3.0 %convolution_convert_fusion.1 = bf16[2560,512]{1,0:T(8,128)(2,1)} fusion(bf16[320,512]{1,0:T(8,128)(2,1)S(1)} %convert_element_type.50, s32[2560]{0:T(1024)S(1)} %copy-done.12), kind=kOutput, calls=%fused_computation.11 | convolution fusion | flops 840990720 | bytes 2959360 | tf_op jit(solution)/shard_map/dot_general | solution.py:69
  44.4 8.1 %all-to-all-done.1 = bf16[128,8,512]{2,1,0:T(8,128)(2,1)} async-done(((bf16[128,8,512]{2,1,0:T(8,128)(2,1)}), bf16[128,8,512]{2,1,0:T(8,128)(2,1)}, u32[]{:S(2)}, u32[]{:S(2)}) %all-to-all-start.1) | async-done | bytes 1048608 | tf_op jit(solution)/shard_map/all_to_all | solution.py:31
  52.6 1.3 pad_maximum_fusion
  53.9 8.2 %gather_fusion.1 = bf16[2560,512]{1,0:T(8,128)(2,1)} fusion(bf16[1344,512]{1,0:T(8,128)(2,1)S(1)} %pad_maximum_fusion, s32[3072]{0:T(1024)S(1)} %pad_clamp_fusion), kind=kCustom, calls=%fused_computation.1 | custom fusion | bytes 5253120 | tf_op jit(solution)/shard_map/gather | solution.py:74
  62.1 5.8 %fusion.61 = f32[2560,512]{1,0:T(8,128)} fusion(bf16[2560,512]{1,0:T(8,128)(2,1)} %gather_fusion.1, bf16[2,1536,512]{2,1,0:T(8,128)(2,1)} %param.22), kind=kOutput, calls=%fused_computation.59 | convolution fusion | flops 1342177280 | bytes 8388608 | tf_op jit(solution)/shard_map/dot_general | solution.py:19
  67.9 11.1 %fusion.92 = (f32[2560]{0:T(1024)S(1)}, f32[2560,512]{0,1:T(8,128)}) fusion(bf16[2,512,512]{2,1,0:T(8,128)(2,1)S(1)} %copy-done.10, f32[2560,512]{1,0:T(8,128)} %fusion.61, f32[2560,512]{1,0:T(8,128)} %fusion.6, bf16[2560,512]{1,0:T(8,128)(2,1)} %convolution_convert_fusion.1, f32[512]{0:T(512)S(1)} %bitcast.121, bf16[2,1536,512]{2,1,0:T(8,128)(2,1)} %param.22), kind=kOutput, calls=%fused_computation.101 | convolution fusion | flops 2696148480 | bytes 19410944 | tf_op jit(solution)/shard_map/dot_general | solution.py:25
  79.0 3.2 %multiply_reduce_fusion.1 = f32[2560]{0:T(1024)S(1)} fusion(f32[2560,512]{0,1:T(8,128)} %get-tuple-element.23, f32[2560]{0:T(1024)S(1)} %broadcast_multiply_fusion.1), kind=kLoop, calls=%fused_computation.8 | loop fusion | flops 3929600 | bytes 5263360 | tf_op jit(solution)/shard_map/reduce_sum | solution.py:11
  83.0 6.3 %select_add_fusion.1 = f32[2560,512]{0,1:T(8,128)} fusion(f32[2560,512]{0,1:T(8,128)} %copy.32, f32[2560,512]{0,1:T(8,128)S(1)} %copy-done.1, f32[512]{0:T(512)S(1)} %bitcast.119, f32[512]{0:T(512)S(1)} %bitcast.118, f32[2560]{0:T(1024)S(1)} %add_rsqrt_fusion.1, f32[2560]{0:T(1024)S(1)} %broadcast_multiply_fusion.1, pred[2560]{0:T(1024)(128)(4,1)S(1)} %fusion.82), kind=kLoop, calls=%fused_computation.7 | loop fusion | flops 7864320 | bytes 15755776 | tf_op jit(solution)/shard_map/add | solution.py:81
  89.3 4.1 %multiply_convert_fusion.3 = bf16[320,512]{1,0:T(8,128)(2,1)S(1)} fusion(f32[320,512]{1,0:T(8,128)S(1)} %copy-done.6, f32[2560,512]{0,1:T(8,128)} %select_add_fusion.1, s32[2560]{0:T(1024)S(1)} %copy-done.12, pred[2560]{0:T(1024)(128)(4,1)S(1)} %fusion.82, bf16[2,1024,512]{2,1,0:T(8,128)(2,1)} %param.27), kind=kOutput, calls=%fused_computation.44 | convolution fusion | flops 1010728960 | bytes 6763008 | tf_op jit(solution)/shard_map/dot_general | solution.py:19
  94.3 5.1 %gather_fusion.2 = bf16[1024,512]{1,0:T(8,128)(2,1)} fusion(bf16[320,512]{1,0:T(8,128)(2,1)S(1)} %fusion.85, s32[1024]{0:T(1024)S(1)} %broadcast_clamp_fusion), kind=kCustom, calls=%fused_computation.2 | custom fusion | bytes 2101248 | tf_op jit(solution)/shard_map/gather | solution.py:30
  99.4 4.1 %all-to-all-start.2 = ((bf16[128,8,512]{2,1,0:T(8,128)(2,1)}), bf16[128,8,512]{2,1,0:T(8,128)(2,1)S(1)}, u32[]{:S(2)}, u32[]{:S(2)}) async-start(bf16[128,8,512]{2,1,0:T(8,128)(2,1)} %bitcast.23), calls=%async_computation.2 | async-start | bytes 2097152 | tf_op jit(solution)/shard_map/all_to_all | solution.py:31
  103.5 2.4 %convolution_add_fusion.1 = f32[320,512]{1,0:T(8,128)} fusion(bf16[320,512]{1,0:T(8,128)(2,1)S(1)} %fusion.85, bf16[2,1024,512]{2,1,0:T(8,128)(2,1)} %param.27, f32[512]{0:T(512)S(1)} %bitcast.114), kind=kOutput, calls=%fused_computation.33 | convolution fusion | flops 167936000 | bytes 1509376 | tf_op jit(solution)/shard_map/dot_general | solution.py:19
  105.9 3.0 %convolution_convert_fusion = bf16[2560,512]{1,0:T(8,128)(2,1)} fusion(bf16[320,512]{1,0:T(8,128)(2,1)S(1)} %fusion.85, s32[2560]{0:T(1024)S(1)} %copy-done.12), kind=kOutput, calls=%fused_computation.10 | convolution fusion | flops 840990720 | bytes 2959360 | tf_op jit(solution)/shard_map/dot_general | solution.py:69
  108.9 4.9 %fusion.16 = f32[2560,512]{1,0:T(8,128)} fusion(f32[2560,512]{0,1:T(8,128)S(1)} %bitcast.99, bf16[2,1536,512]{2,1,0:T(8,128)(2,1)} %param.22), kind=kOutput, calls=%fused_computation.29 | convolution fusion | flops 1343488000 | bytes 11010048 | tf_op jit(solution)/shard_map/dot_general | solution.py:19
  113.9 9.5 %all-to-all-done.2 = bf16[128,8,512]{2,1,0:T(8,128)(2,1)S(1)} async-done(((bf16[128,8,512]{2,1,0:T(8,128)(2,1)}), bf16[128,8,512]{2,1,0:T(8,128)(2,1)S(1)}, u32[]{:S(2)}, u32[]{:S(2)}) %all-to-all-start.2) | async-done | bytes 1048608 | tf_op jit(solution)/shard_map/all_to_all | solution.py:31
  123.4 1.0 copy-done.2
  124.4 1.3 pad_maximum_fusion.1
  125.7 8.2 %gather_fusion.3 = bf16[2560,512]{1,0:T(8,128)(2,1)} fusion(bf16[1344,512]{1,0:T(8,128)(2,1)S(1)} %pad_maximum_fusion.1, s32[3072]{0:T(1024)S(1)} %pad_clamp_fusion), kind=kCustom, calls=%fused_computation.3 | custom fusion | bytes 5253120 | tf_op jit(solution)/shard_map/gather | solution.py:74
  133.9 5.8 %fusion.51 = f32[2560,512]{1,0:T(8,128)} fusion(bf16[2560,512]{1,0:T(8,128)(2,1)} %gather_fusion.3, bf16[2,1536,512]{2,1,0:T(8,128)(2,1)} %param.22), kind=kOutput, calls=%fused_computation.50 | convolution fusion | flops 1342177280 | bytes 8388608 | tf_op jit(solution)/shard_map/dot_general | solution.py:19
  139.7 11.1 %fusion.96 = (f32[2560]{0:T(1024)S(1)}, f32[2560,512]{0,1:T(8,128)}) fusion(bf16[2,512,512]{2,1,0:T(8,128)(2,1)S(1)} %copy-done.11, f32[2560,512]{1,0:T(8,128)} %fusion.51, f32[2560,512]{1,0:T(8,128)} %fusion.16, bf16[2560,512]{1,0:T(8,128)(2,1)} %convolution_convert_fusion, f32[512]{0:T(512)S(1)} %bitcast.120, bf16[2,1536,512]{2,1,0:T(8,128)(2,1)} %param.22), kind=kOutput, calls=%fused_computation.103 | convolution fusion | flops 2696148480 | bytes 19410944 | tf_op jit(solution)/shard_map/dot_general | solution.py:25
  150.8 3.2 %multiply_reduce_fusion = f32[2560]{0:T(1024)S(1)} fusion(f32[2560,512]{0,1:T(8,128)} %get-tuple-element.27, f32[2560]{0:T(1024)S(1)} %broadcast_multiply_fusion), kind=kLoop, calls=%fused_computation.5 | loop fusion | flops 3929600 | bytes 5263360 | tf_op jit(solution)/shard_map/reduce_sum | solution.py:11
  154.0 0.8 copy-done
  154.8 6.2 %select_add_fusion = f32[2560,512]{0,1:T(8,128)} fusion(f32[2560,512]{0,1:T(8,128)} %select_add_fusion.1, f32[2560,512]{0,1:T(8,128)S(1)} %copy-done, f32[512]{0:T(512)S(1)} %bitcast.117, f32[512]{0:T(512)S(1)} %bitcast.116, f32[2560]{0:T(1024)S(1)} %add_rsqrt_fusion, f32[2560]{0:T(1024)S(1)} %broadcast_multiply_fusion, pred[2560]{0:T(1024)(128)(4,1)S(1)} %fusion.82), kind=kLoop, calls=%fused_computation.4 | loop fusion | flops 7864320 | bytes 15755776 | tf_op jit(solution)/shard_map/add | solution.py:81
  161.0 5.9 %copy.33 = f32[2560,512]{1,0:T(8,128)} copy(f32[2560,512]{0,1:T(8,128)} %select_add_fusion) | data formatting | bytes 10485760
  166.9 4.1 %multiply_convert_fusion.2 = bf16[320,512]{1,0:T(8,128)(2,1)S(1)} fusion(f32[320,512]{1,0:T(8,128)S(1)} %copy-done.5, f32[2560,512]{0,1:T(8,128)} %select_add_fusion, s32[2560]{0:T(1024)S(1)} %copy-done.12, pred[2560]{0:T(1024)(128)(4,1)S(1)} %fusion.82, bf16[2,1024,512]{2,1,0:T(8,128)(2,1)} %param.27), kind=kOutput, calls=%fused_computation.41 | convolution fusion | flops 1010728960 | bytes 6763008 | tf_op jit(solution)/shard_map/dot_general | solution.py:19
  171.7 1.1 add_add_fusion
  (60 shorter events, 7.5 us)
Async XLA Ops:
  0.6 14.8 %all-to-all-start = ((f32[2,320,256]{2,1,0:T(8,128)}), f32[2,320,256]{2,1,0:T(8,128)S(1)}, u32[]{:S(2)}, u32[]{:S(2)}) async-start(f32[2,320,256]{2,1,0:T(8,128)} %bitcast.107), calls=%async_computation | async-start | bytes 1310720 | tf_op jit(solution)/shard_map/all_to_all | solution.py:59
  8.9 6.4 %copy-start.9 = (s32[20]{0:T(128)S(1)}, s32[20]{0:T(128)}, u32[]{:S(2)}) copy-start(s32[20]{0:T(128)} %param.20) | copy-start | bytes 244
  8.9 6.5 %copy-start.7 = (s32[2560]{0:T(1024)S(1)}, s32[2560]{0:T(1024)}, u32[]{:S(2)}) copy-start(s32[2560]{0:T(1024)} %param.18) | copy-start | bytes 30724
  20.7 31.9 %all-to-all-start.1 = ((bf16[128,8,512]{2,1,0:T(8,128)(2,1)}), bf16[128,8,512]{2,1,0:T(8,128)(2,1)}, u32[]{:S(2)}, u32[]{:S(2)}) async-start(bf16[128,8,512]{2,1,0:T(8,128)(2,1)} %bitcast.104), calls=%async_computation.1 | async-start | bytes 2097152 | tf_op jit(solution)/shard_map/all_to_all | solution.py:31
  33.2 5.9 %copy-start.8 = (f32[2,512]{1,0:T(2,128)S(1)}, f32[2,512]{1,0:T(2,128)}, u32[]{:S(2)}) copy-start(f32[2,512]{1,0:T(2,128)} %param.31) | copy-start | bytes 12292
  33.2 8.2 %copy-start.12 = (s32[2560]{0:T(1024)S(1)}, s32[2560]{0:T(1024)}, u32[]{:S(2)}) copy-start(s32[2560]{0:T(1024)} %param.19) | copy-start | bytes 30724
  62.1 5.8 %copy-start.10 = (bf16[2,512,512]{2,1,0:T(8,128)(2,1)S(1)}, bf16[2,512,512]{2,1,0:T(8,128)(2,1)}, u32[]{:S(2)}) copy-start(bf16[2,512,512]{2,1,0:T(8,128)(2,1)} %param.24) | copy-start | bytes 3145732
  78.9 4.0 %copy-start.1 = (f32[2560,512]{0,1:T(8,128)S(1)}, f32[2560,512]{0,1:T(8,128)}, u32[]{:S(2)}) copy-start(f32[2560,512]{0,1:T(8,128)} %get-tuple-element.23) | copy-start | bytes 15728644
  83.0 6.3 %copy-start.6 = (f32[320,512]{1,0:T(8,128)S(1)}, f32[320,512]{1,0:T(8,128)}, u32[]{:S(2)}) copy-start(f32[320,512]{1,0:T(8,128)} %convolution_add_fusion.3) | copy-start | bytes 1966084
  89.3 4.1 %copy-start.3 = (bf16[2,512,512]{2,1,0:T(8,128)(2,1)S(1)}, bf16[2,512,512]{2,1,0:T(8,128)(2,1)}, u32[]{:S(2)}) copy-start(bf16[2,512,512]{2,1,0:T(8,128)(2,1)} %param.29) | copy-start | bytes 3145732
  99.4 24.0 %all-to-all-start.2 = ((bf16[128,8,512]{2,1,0:T(8,128)(2,1)}), bf16[128,8,512]{2,1,0:T(8,128)(2,1)S(1)}, u32[]{:S(2)}, u32[]{:S(2)}) async-start(bf16[128,8,512]{2,1,0:T(8,128)(2,1)} %bitcast.23), calls=%async_computation.2 | async-start | bytes 2097152 | tf_op jit(solution)/shard_map/all_to_all | solution.py:31
  103.5 5.4 %slice-start = ((s8[5242880]{0:T(1024)(128)(4,1)}), s8[4194304]{0:T(1024)(128)(4,1)S(1)}, s32[]{:S(2)}) async-start(s8[5242880]{0:T(1024)(128)(4,1)} %bitcast.98), calls=%async_computation.3 | async-start | bytes 8388608
  105.9 3.1 %slice-start.1 = ((s8[5242880]{0:T(1024)(128)(4,1)}), s8[1048576]{0:T(1024)(128)(4,1)S(1)}, s32[]{:S(2)}) async-start(s8[5242880]{0:T(1024)(128)(4,1)} %bitcast.98), calls=%async_computation.4 | async-start | bytes 2097152
  123.4 1.0 copy-start.2
  133.9 5.8 %copy-start.11 = (bf16[2,512,512]{2,1,0:T(8,128)(2,1)S(1)}, bf16[2,512,512]{2,1,0:T(8,128)(2,1)}, u32[]{:S(2)}) copy-start(bf16[2,512,512]{2,1,0:T(8,128)(2,1)} %param.24) | copy-start | bytes 3145732
  150.8 4.0 %copy-start = (f32[2560,512]{0,1:T(8,128)S(1)}, f32[2560,512]{0,1:T(8,128)}, u32[]{:S(2)}) copy-start(f32[2560,512]{0,1:T(8,128)} %get-tuple-element.27) | copy-start | bytes 15728644
  161.0 5.9 %copy-start.5 = (f32[320,512]{1,0:T(8,128)S(1)}, f32[320,512]{1,0:T(8,128)}, u32[]{:S(2)}) copy-start(f32[320,512]{1,0:T(8,128)} %convolution_add_fusion.1) | copy-start | bytes 1966084
  166.9 4.1 %copy-start.4 = (bf16[2,512,512]{2,1,0:T(8,128)(2,1)S(1)}, bf16[2,512,512]{2,1,0:T(8,128)(2,1)}, u32[]{:S(2)}) copy-start(bf16[2,512,512]{2,1,0:T(8,128)(2,1)} %param.29) | copy-start | bytes 3145732
where the time goes:
time: 174 us; the launch traced here: 173 us
  matrix products  64.8 us (37%)
  local copies, waits for them, and re-layouts  45.2 us (26%)
  other arithmetic  24.3 us (14%)
  starting transfers between devices  20.1 us (12%)
  waiting for transfers between devices  17.6 us (10%)
    dot_general x8, matrix products, perceptron(): jnp.dot(pieces[position], first_weight[position * columns:(position + 1)...  35.6 us
    dot_general x4, matrix products, perceptron(): result = jnp.dot(active, second_weight, preferred_element_type=jnp.float32)  23 us
    all_to_all x2, waiting for transfers between devices, fetch_halo(): lax.all_to_all(outgoing, ('patch', 'band'), split_axis=0, concat_axis=0,...  17.6 us
    all_to_all x2, starting transfers between devices, fetch_halo(): lax.all_to_all(outgoing, ('patch', 'band'), split_axis=0, concat_axis=0,...  16.6 us
    gather x2, local copies, waits for them, and re-layouts, shards(): sender_table[edge_sender]  16.4 us
    unnamed x32, local copies, waits for them, and re-layouts  14.5 us
    add x2, other arithmetic, shards(): edge_state + jnp.where(usable[:, None], update, jnp.zeros_like(update))  12.5 us
    gather x2, local copies, waits for them, and re-layouts, fetch_halo(): outgoing = node_low[send_lists]  10.2 us
  transfers between devices with their start and end apart: 3, of which 2 were waited for; matrix products, arithmetic and copies ran while one was open for 19% of the time, Pallas kernels for 0%

commit v1 on v0

v1 whole, which is shorter than its diff:
```python
import functools

import jax
import jax.numpy as jnp
from jax import lax
from jax.experimental import pallas as pl
from jax.experimental.pallas import tpu as pltpu
from jax.sharding import PartitionSpec as P

MESH = pl.DeviceIdType.MESH
F32 = jnp.float32
BF16 = jnp.bfloat16
D = 512
HALF = 256
ROWS = 320
EDGE = 2560
BLK = 256
NBLK = EDGE // BLK
EPS = 1e-05


def dot(a, b):
    return jnp.dot(a, b, preferred_element_type=F32)


def swish(v):
    half = 0.5 * v
    return half + half * jnp.tanh(half)


def norm(v, gain, offset):
    centre = v - jnp.sum(v, axis=-1, keepdims=True) * (1.0 / D)
    spread = jnp.sum(centre * centre, axis=-1, keepdims=True) * (1.0 / D)
    return centre * lax.rsqrt(spread + EPS) * gain + offset


def column(row):
    return jnp.transpose(jnp.broadcast_to(row, (128, 128)))


def hot(match):
    return jnp.where(match, 1.0, 0.0).astype(BF16)


def lanes(base):
    return (lax.broadcasted_iota(jnp.int32, (128, 128), 1) + base).astype(F32)


def edge_finish(pre, state, usable, w2, gain, offset):
    hidden = swish(pre).astype(BF16)
    update = norm(dot(hidden, w2), gain, offset)
    return state + jnp.where(usable, update, 0.0)


def usable_rows(counts, block):
    row = lax.broadcasted_iota(jnp.int32, (128, 1), 0)
    return jnp.concatenate([row < counts[2 * block], row < counts[2 * block + 1]], axis=0)


def summing(rcv, counts, block):
    node = lax.broadcasted_iota(jnp.int32, (ROWS, 128), 0)
    lane = lax.broadcasted_iota(jnp.int32, (1, 128), 1)
    parts = []
    for j in range(2):
        i = 2 * block + j
        target = jnp.where(lane < counts[i], rcv[pl.ds(i, 1), :], -1)
        parts.append(hot(node == target))
    return jnp.concatenate(parts, axis=1)


def node_finish(pv, summed, v1, w2, gain, offset):
    hidden = swish(pv + dot(summed.astype(BF16), v1)).astype(BF16)
    return norm(dot(hidden, w2), gain, offset)


def place():
    p = lax.axis_index("patch")
    b = lax.axis_index("band")
    core = p % 2
    z = (p // 2) % 4
    x = ((p // 8) % 2) * 2 + b
    y = p // 16
    return p, b, core, x, y, z


def at(core, x, y, z):
    return ((y * 2 + x // 2) * 4 + z) * 2 + core, x % 2


def turn(k):
    return k + (k // 2) * (1 - 2 * (k % 2))


def first_kernel(
    latents,
    edges,
    snd,
    rcv,
    counts,
    lists,
    we1,
    eb1,
    we2,
    egain,
    eoff,
    wn1,
    nb1,
    wn2,
    ngain,
    noff,
    pre_out,
    edge_out,
    node_out,
    pv_out,
    table_out,
    lat,
    state,
    pre,
    hot_local,
    hot_halo,
    hot_sum,
    hot_send,
    w1,
    w2,
    v1,
    v2,
    band_out,
    band_in,
    node,
    low,
    table,
    stage,
    recv,
    total,
    lat_sem,
    edge_sem,
    w_sem,
    band_send,
    band_recv,
    halo_send,
    halo_recv,
    out_sem,
    greet,
):
    p, b, core, x, y, z = place()
    me = p * 2 + b
    barrier = pltpu.get_barrier_semaphore()
    plane = [(0, 0, dy, dz) for dy in range(4) for dz in range(4) if (dy, dz) != (0, 0)]
    line = [(dc, dx, 0, 0) for dc in range(2) for dx in range(4) if (dc, dx) != (0, 0)]

    def peer(dc, dx, dy, dz):
        return at((core + dc) % 2, (x + dx) % 4, (y + dy) % 4, (z + dz) % 4)

    for o in plane + line:
        pl.semaphore_signal(barrier, inc=1, device_id=peer(*o), device_id_type=MESH)
    lat_copy = pltpu.make_async_copy(latents, lat, lat_sem)
    lat_copy.start()
    w_copies = [
        pltpu.make_async_copy(we1, w1, w_sem.at[0]),
        pltpu.make_async_copy(wn1, v1, w_sem.at[1]),
        pltpu.make_async_copy(we2.at[0], w2, w_sem.at[2]),
        pltpu.make_async_copy(wn2.at[0], v2, w_sem.at[3]),
    ]
    w_copies[0].start()
    edge_copies = [
        pltpu.make_async_copy(edges.at[pl.ds(i * 512, 512)], state.at[pl.ds(i * 512, 512)], edge_sem.at[i])
        for i in range(EDGE // 512)
    ]
    for c in edge_copies:
        c.start()
    for c in w_copies[1:]:
        c.start()
    lat_copy.wait()
    band_out[...] = lat[pl.ds((1 - b) * ROWS, ROWS), :].astype(BF16)

    for c in range(8):
        block = jnp.concatenate(
            [jnp.broadcast_to(lists[:, q : q + 1], (8, 128)) for q in range(16 * c, 16 * c + 16)], axis=0
        ).astype(F32)
        for t in range(3):
            wide = 128 if t < 2 else 64
            hot_send[c, :, t * 128 : t * 128 + wide] = hot(block == lanes(t * 128))[:, :wide]

    pl.semaphore_wait(barrier, len(plane) + len(line))
    for o in line:
        pl.semaphore_signal(greet, inc=1, device_id=peer(*o), device_id_type=MESH)
    pl.semaphore_wait(greet, len(line))
    band_copy = pltpu.make_async_remote_copy(
        src_ref=band_out,
        dst_ref=band_in,
        send_sem=band_send,
        recv_sem=band_recv,
        device_id=(p, 1 - b),
        device_id_type=MESH,
    )
    band_copy.start()

    def hots(i, _):
        rows = pl.ds(pl.multiple_of(i * 128, 128), 128)
        s = column(snd[pl.ds(i, 1), :].astype(F32))
        r = column(rcv[pl.ds(i, 1), :].astype(F32)) + float(ROWS)
        lane = lax.broadcasted_iota(jnp.int32, (128, 128), 1)
        mixed = jnp.where(lane < 64, s, r)
        for t, source in enumerate((s, s, mixed, r, r)):
            hot_local[rows, t * 128 : t * 128 + 128] = hot(source == lanes(t * 128))
        for t in range(8):
            hot_halo[t // 2, rows, (t % 2) * 128 : (t % 2) * 128 + 128] = hot(s == lanes(ROWS + t * 128))
        return 0

    lax.fori_loop(0, EDGE // 128, hots, 0)

    def sums(i, _):
        hot_sum[i] = summing(rcv, counts, i)
        return 0

    lax.fori_loop(0, NBLK, sums, 0)
    w_copies[0].wait()
    for c in edge_copies:
        c.wait()

    def edge_part(layer):
        def body(i, _):
            rows = pl.ds(pl.multiple_of(i * BLK, BLK), BLK)
            pre[rows, :] = dot(state[rows, :].astype(BF16), w1[layer, :D, :]) + eb1[pl.ds(layer, 1), :]
            return 0

        lax.fori_loop(0, NBLK, body, 0)

    edge_part(0)
    band_copy.wait()
    own = lat[pl.ds(b * ROWS, ROWS), :]
    other = band_in[...].astype(F32)
    node[:, :HALF] = jnp.where(b == 0, own, other)
    node[:, HALF:] = jnp.where(b == 0, other, own)
    for c in w_copies[1:]:
        c.wait()

    def exchange(layer):
        low[...] = node[...].astype(BF16)
        table[:ROWS, :] = dot(low[...], w1[layer, D : 2 * D, :]).astype(BF16)

        def fill(c, _):
            rows = dot(hot_send[c], table[:ROWS, :]).astype(BF16)
            stage[layer, pl.ds(c * 16, 16)] = rows.reshape(16, 8, D)
            return 0

        lax.fori_loop(0, 8, fill, 0)
        recv[layer, me] = stage[layer, me]

        def send(k, _):
            px, bx = at((core + k) % 2, (x + k // 2) % 4, (y + turn(k // 32)) % 4, (z + k // 8) % 4)
            pltpu.make_async_remote_copy(
                src_ref=stage.at[layer, px * 2 + bx],
                dst_ref=recv.at[layer, me],
                send_sem=halo_send.at[layer],
                recv_sem=halo_recv.at[layer, k // 32],
                device_id=(px, bx),
                device_id_type=MESH,
            ).start()
            return 0

        lax.fori_loop(1, 128, send, 0)
        table[ROWS:, :] = dot(low[...], w1[layer, 2 * D :, :]).astype(BF16)
        pv_out[...] = dot(low[...], v1[layer, :D, :]) + nb1[pl.ds(layer, 1), :]

    def local_part():
        def body(i, _):
            rows = pl.ds(pl.multiple_of(i * BLK, BLK), BLK)
            pre[rows, :] += dot(hot_local[rows, :], table[...])
            return 0

        lax.fori_loop(0, NBLK, body, 0)

    def wait_chunk(layer, c):
        n = 31 if c == 0 else 32
        pltpu.make_async_copy(
            stage.at[layer, pl.ds(0, n)], recv.at[layer, pl.ds(0, n)], halo_recv.at[layer, c]
        ).wait()
        return (y - (0, 1, 3, 2)[c] + 4) % 4

    def chunk_rows(layer, source):
        return recv[layer, pl.ds(source * 32, 32)].reshape(256, D)

    def halo_part(layer, c):
        source = wait_chunk(layer, c)

        def body(i, _):
            rows = pl.ds(pl.multiple_of(i * BLK, BLK), BLK)
            pre[rows, :] += dot(hot_halo[source, rows, :], chunk_rows(layer, source))
            return 0

        lax.fori_loop(0, NBLK, body, 0)

    def wait_sends(layer):
        pltpu.make_async_copy(
            stage.at[layer, pl.ds(0, 127)], recv.at[layer, pl.ds(0, 127)], halo_send.at[layer]
        ).wait()

    exchange(0)
    local_part()
    for c in range(3):
        halo_part(0, c)
    source = wait_chunk(0, 3)
    total[...] = jnp.zeros_like(total)

    def finish(i, _):
        rows = pl.ds(pl.multiple_of(i * BLK, BLK), BLK)
        value = pre[rows, :] + dot(hot_halo[source, rows, :], chunk_rows(0, source))
        done = edge_finish(value, state[rows, :], usable_rows(counts, i), w2[...], egain[0:1, :], eoff[0:1, :])
        state[rows, :] = done
        total[...] += dot(hot_sum[i], done.astype(BF16))
        return 0

    lax.fori_loop(0, NBLK, finish, 0)
    edge_copy = pltpu.make_async_copy(state, edge_out, out_sem.at[0])
    edge_copy.start()
    node[...] += node_finish(pv_out[...], total[...], v1[0, D:, :], v2[...], ngain[0:1, :], noff[0:1, :])
    wait_sends(0)
    exchange(1)
    node_out[...] = node[...]
    edge_part(1)
    local_part()
    for c in range(3):
        halo_part(1, c)
    pre_copy = pltpu.make_async_copy(pre, pre_out, out_sem.at[1])
    pre_copy.start()
    source = wait_chunk(1, 3)
    table_out[...] = chunk_rows(1, source)
    wait_sends(1)
    edge_copy.wait()
    pre_copy.wait()


def second_kernel(
    pre, state, snd, rcv, counts, table, node, pv, we2, egain, eoff, wn1, wn2, ngain, noff, edge_out, node_out, total
):
    i = pl.program_id(0)
    y = lax.axis_index("patch") // 16
    base = ROWS + ((y - 2 + 4) % 4) * 256
    halves = []
    for j in range(2):
        s = column(snd[pl.ds(2 * i + j, 1), :].astype(F32))
        halves.append(jnp.concatenate([hot(s == lanes(base + t * 128)) for t in range(2)], axis=1))
    value = pre[...] + dot(jnp.concatenate(halves, axis=0), table[...])
    done = edge_finish(value, state[...], usable_rows(counts, i), we2[...], egain[1:2, :], eoff[1:2, :])
    edge_out[...] = done

    @pl.when(i == 0)
    def _():
        total[...] = jnp.zeros_like(total)

    total[...] += dot(summing(rcv, counts, i), done.astype(BF16))

    @pl.when(i == NBLK - 1)
    def _():
        node_out[...] = node[...] + node_finish(pv[...], total[...], wn1[...], wn2[...], ngain[1:2, :], noff[1:2, :])


VMEM = pl.BlockSpec(memory_space=pltpu.VMEM)
SMEM = pl.BlockSpec(memory_space=pltpu.SMEM)
ANY = pl.BlockSpec(memory_space=pl.ANY)


def shards(
    latents,
    edge_latents,
    edge_sender,
    edge_receiver,
    block_counts,
    send_rows,
    edge_first_weight,
    edge_first_bias,
    edge_second_weight,
    edge_gain,
    edge_offset,
    node_first_weight,
    node_first_bias,
    node_second_weight,
    node_gain,
    node_offset,
):
    snd = edge_sender.reshape(EDGE // 128, 128)
    rcv = edge_receiver.reshape(EDGE // 128, 128)
    lists = jnp.transpose(send_rows[0])
    shape = jax.ShapeDtypeStruct
    pre, state, node, pv, table = pl.pallas_call(
        first_kernel,
        out_shape=(
            shape((EDGE, D), F32),
            shape((EDGE, D), F32),
            shape((ROWS, D), F32),
            shape((ROWS, D), F32),
            shape((256, D), BF16),
        ),
        in_specs=[ANY, ANY, VMEM, VMEM, SMEM, VMEM, ANY, VMEM, ANY, VMEM, VMEM, ANY, VMEM, ANY, VMEM, VMEM],
        out_specs=(ANY, ANY, VMEM, VMEM, VMEM),
        scratch_shapes=[
            pltpu.VMEM((2 * ROWS, HALF), F32),
            pltpu.VMEM((EDGE, D), F32),
            pltpu.VMEM((EDGE, D), F32),
            pltpu.VMEM((EDGE, 2 * ROWS), BF16),
            pltpu.VMEM((4, EDGE, 256), BF16),
            pltpu.VMEM((NBLK, ROWS, BLK), BF16),
            pltpu.VMEM((8, 128, ROWS), BF16),
            pltpu.VMEM((2, 3 * D, D), BF16),
            pltpu.VMEM((D, D), BF16),
            pltpu.VMEM((2, 2 * D, D), BF16),
            pltpu.VMEM((D, D), BF16),
            pltpu.VMEM((ROWS, HALF), BF16),
            pltpu.VMEM((ROWS, HALF), BF16),
            pltpu.VMEM((ROWS, D), F32),
            pltpu.VMEM((ROWS, D), BF16),
            pltpu.VMEM((2 * ROWS, D), BF16),
            pltpu.VMEM((2, 128, 8, D), BF16),
            pltpu.VMEM((2, 128, 8, D), BF16),
            pltpu.VMEM((ROWS, D), F32),
            pltpu.SemaphoreType.DMA,
            pltpu.SemaphoreType.DMA((EDGE // 512,)),
            pltpu.SemaphoreType.DMA((4,)),
            pltpu.SemaphoreType.DMA,
            pltpu.SemaphoreType.DMA,
            pltpu.SemaphoreType.DMA((2,)),
            pltpu.SemaphoreType.DMA((2, 4)),
            pltpu.SemaphoreType.DMA((2,)),
            pltpu.SemaphoreType.REGULAR,
        ],
        compiler_params=pltpu.CompilerParams(
            collective_id=0, has_side_effects=True, vmem_limit_bytes=56 * 1024 * 1024
        ),
    )(
        latents,
        edge_latents,
        snd,
        rcv,
        block_counts,
        lists,
        edge_first_weight,
        edge_first_bias,
        edge_second_weight,
        edge_gain,
        edge_offset,
        node_first_weight,
        node_first_bias,
        node_second_weight,
        node_gain,
        node_offset,
    )

    def whole(*dims):
        return pl.BlockSpec(dims, lambda i: (0,) * len(dims))

    new_edges, new_nodes = pl.pallas_call(
        second_kernel,
        grid=(NBLK,),
        out_shape=(shape((EDGE, D), F32), shape((ROWS, D), F32)),
        in_specs=[
            pl.BlockSpec((BLK, D), lambda i: (i, 0)),
            pl.BlockSpec((BLK, D), lambda i: (i, 0)),
            whole(EDGE // 128, 128),
            whole(EDGE // 128, 128),
            SMEM,
            whole(256, D),
            whole(ROWS, D),
            whole(ROWS, D),
            pl.BlockSpec((None, D, D), lambda i: (1, 0, 0)),
            whole(2, D),
            whole(2, D),
            pl.BlockSpec((None, D, D), lambda i: (1, 1, 0)),
            pl.BlockSpec((None, D, D), lambda i: (1, 0, 0)),
            whole(2, D),
            whole(2, D),
        ],
        out_specs=(pl.BlockSpec((BLK, D), lambda i: (i, 0)), whole(ROWS, D)),
        scratch_shapes=[pltpu.VMEM((ROWS, D), F32)],
        compiler_params=pltpu.CompilerParams(vmem_limit_bytes=40 * 1024 * 1024),
    )(
        pre,
        state,
        snd,
        rcv,
        block_counts,
        table,
        node,
        pv,
        edge_second_weight,
        edge_gain,
        edge_offset,
        node_first_weight,
        node_second_weight,
        node_gain,
        node_offset,
    )
    return new_nodes, new_edges


def solution(mesh):
    split = P(("patch", "band"))
    return jax.shard_map(
        shards,
        mesh=mesh,
        in_specs=(
            P("patch", "band"),
            P(("patch", "band"), None),
            split,
            split,
            split,
            P(("patch", "band"), None, None),
        )
        + (P(),) * 10,
        out_specs=(P(("patch", "band"), None), P(("patch", "band"), None)),
        check_vma=False,
    )
```

time: 174 us -> 97.1 us (0.56)
  Pallas kernels: 0 us -> 90.1 us
  matrix products: 64.8 us -> 0 us
  local copies, waits for them, and re-layouts: 45.2 us -> 5.64 us
  other arithmetic: 24.3 us -> 0 us
  starting transfers between devices: 20.1 us -> 0 us
  waiting for transfers between devices: 17.6 us -> 0 us
    pallas_call x0 -> x2, Pallas kernels: none -> 90.1 us  [the longest x1 75.9 us: shards(): pl.pallas_call(first_kernel, out_shape=(shape((EDGE, D), F32), shape((EDG...]
    dot_general x14 -> x0, matrix products: 64.8 us -> none  [the longest x8 35.6 us: perceptron(): jnp.dot(pieces[position], first_weight[position * columns:(position + 1)...]
    gather x4 -> x0, local copies, waits for them, and re-layouts: 26.6 us -> none  [the longest x2 16.4 us: shards(): sender_table[edge_sender]]
    all_to_all x3 -> x0, starting transfers between devices: 20.1 us -> none  [the longest x2 16.6 us: fetch_halo(): lax.all_to_all(outgoing, ('patch', 'band'), split_axis=0, concat_axis=0,...]
    all_to_all x3 -> x0, waiting for transfers between devices: 17.6 us -> none  [the longest x2 17.6 us: fetch_halo(): lax.all_to_all(outgoing, ('patch', 'band'), split_axis=0, concat_axis=0,...]
    add x3 -> x0, other arithmetic: 13.6 us -> none  [the longest x2 12.5 us: shards(): edge_state + jnp.where(usable[:, None], update, jnp.zeros_like(update))]
    unnamed x32 -> x28, local copies, waits for them, and re-layouts: 14.5 us -> 5.64 us
    reduce_sum x4 -> x0, other arithmetic: 6.93 us -> none  [layer_norm(): spread = jnp.mean(centre * centre, axis=-1, keepdims=True)]
  transfers between devices with their start and end apart: 3 -> 0, of which waited for: 2 -> 0; matrix products, arithmetic and copies ran while one was open for 19% -> 0% of each run, Pallas kernels for 0% -> 0%
where the time goes in v1:
time: 97.1 us; the launch traced here: 96.5 us
  Pallas kernels  90.1 us (93%)
  local copies, waits for them, and re-layouts  5.64 us (6%)
    pallas_call x1, Pallas kernels, shards(): pl.pallas_call(first_kernel, out_shape=(shape((EDGE, D), F32), shape((EDG...  75.9 us
    pallas_call x1, Pallas kernels, shards(): pl.pallas_call(second_kernel, grid=(NBLK,), out_shape=(shape((EDGE, D), F...  14.2 us
    unnamed x28, local copies, waits for them, and re-layouts  5.64 us

profile of v1, /device:TPU:1, one launch (start us, length us, event | category | flops | bytes accessed | tf_op | source)
XLA Modules:
  0.0 96.5 jit_solution(4550136412759031339)
XLA Ops:
  0.6 0.0 copy-start
  0.6 0.0 copy-start.2
  0.7 0.0 copy-start.3
  0.7 0.0 copy-start.7
  0.7 0.0 copy-start.8
  0.7 0.0 copy-start.9
  0.7 0.0 copy-start.10
  0.7 0.0 copy-start.11
  0.7 0.0 copy-start.12
  0.7 0.0 copy-start.13
  0.7 75.9 %shard_map.167 = (f32[2560,512]{1,0:T(8,128)}, f32[2560,512]{1,0:T(8,128)}, f32[320,512]{1,0:T(8,128)}, f32[320,512]{1,0:T(8,128)}, bf16[256,512]{1,0:T(8,128)(2,1)}) custom-call(f32[640,256]{1,0:T(8,128)} %latents.1, f32[2560,512]{1,0:T(8,128)} %edges.1, s32[20,128]{1,0:T(8,128)} %bitcast.5, s32[20,128]{1,0:T(8,128)} %bitcast.7, s32[20]{0:T(128)} %counts.3, ...), custom_call_target="tpu_custom_call" | custom-call | tf_op jit(solution)/shard_map/pallas_call | solution.py:386
  76.7 0.0 copy-done
  76.7 0.0 copy-done.2
  76.7 0.0 copy-done.3
  76.7 0.0 copy-done.7
  76.7 0.0 copy-done.8
  76.7 0.0 copy-done.9
  76.7 0.0 copy-done.10
  76.7 0.0 copy-done.11
  76.7 0.0 copy-done.12
  76.7 0.0 copy-done.13
  76.8 0.0 copy-start.1
  76.8 2.5 %copy-done.1 = f32[2560,512]{1,0:T(8,128)S(1)} copy-done((f32[2560,512]{1,0:T(8,128)S(1)}, f32[2560,512]{1,0:T(8,128)}, u32[]{:S(2)}) %copy-start.1) | copy-done | bytes 5242904
  79.2 0.0 copy-start.4
  79.2 1.1 %copy-done.4 = f32[320,512]{1,0:T(8,128)S(1)} copy-done((f32[320,512]{1,0:T(8,128)S(1)}, f32[320,512]{1,0:T(8,128)}, u32[]{:S(2)}) %copy-start.4) | copy-done | bytes 655384
  80.3 0.0 copy-start.5
  80.3 1.1 %copy-done.5 = f32[320,512]{1,0:T(8,128)S(1)} copy-done((f32[320,512]{1,0:T(8,128)S(1)}, f32[320,512]{1,0:T(8,128)}, u32[]{:S(2)}) %copy-start.5) | copy-done | bytes 655384
  81.4 0.0 copy-start.6
  81.4 0.9 copy-done.6
  82.4 14.2 %shard_map.168 = (f32[2560,512]{1,0:T(8,128)}, f32[320,512]{1,0:T(8,128)}) custom-call(f32[2560,512]{1,0:T(8,128)S(1)} %copy-done.1, f32[2560,512]{1,0:T(8,128)} %get-tuple-element.10.state, s32[20,128]{1,0:T(8,128)S(1)} %bitcast.6, s32[20,128]{1,0:T(8,128)S(1)} %bitcast.8, s32[20]{0:T(128)S(1)} %copy-done.13, bf16[256,512]{1,0:T(8,128)(2,1)S(1)} %copy-done.6, ...), custom_call_target="tpu_custom_call" | custom-call | tf_op jit(solution)/shard_map/pallas_call | solution.py:452
Async XLA Ops:
  0.6 76.0 %copy-start = (bf16[2,1024,512]{2,1,0:T(8,128)(2,1)S(1)}, bf16[2,1024,512]{2,1,0:T(8,128)(2,1)}, u32[]{:S(2)}) copy-start(bf16[2,1024,512]{2,1,0:T(8,128)(2,1)} %wn1.3) | copy-start | bytes 6291460
  0.6 76.0 %copy-start.2 = (bf16[2,512,512]{2,1,0:T(8,128)(2,1)S(1)}, bf16[2,512,512]{2,1,0:T(8,128)(2,1)}, u32[]{:S(2)}) copy-start(bf16[2,512,512]{2,1,0:T(8,128)(2,1)} %we2.3) | copy-start | bytes 3145732
  0.7 76.0 %copy-start.3 = (bf16[2,512,512]{2,1,0:T(8,128)(2,1)S(1)}, bf16[2,512,512]{2,1,0:T(8,128)(2,1)}, u32[]{:S(2)}) copy-start(bf16[2,512,512]{2,1,0:T(8,128)(2,1)} %wn2.3) | copy-start | bytes 3145732
  0.7 76.0 %copy-start.7 = (s32[2560]{0:T(1024)S(1)}, s32[2560]{0:T(1024)}, u32[]{:S(2)}) copy-start(s32[2560]{0:T(1024)} %param.18) | copy-start | bytes 30724
  0.7 76.0 %copy-start.8 = (s32[2560]{0:T(1024)S(1)}, s32[2560]{0:T(1024)}, u32[]{:S(2)}) copy-start(s32[2560]{0:T(1024)} %param.19) | copy-start | bytes 30724
  0.7 76.0 %copy-start.9 = (f32[2,512]{1,0:T(2,128)S(1)}, f32[2,512]{1,0:T(2,128)}, u32[]{:S(2)}) copy-start(f32[2,512]{1,0:T(2,128)} %egain.3) | copy-start | bytes 12292
  0.7 76.0 %copy-start.10 = (f32[2,512]{1,0:T(2,128)S(1)}, f32[2,512]{1,0:T(2,128)}, u32[]{:S(2)}) copy-start(f32[2,512]{1,0:T(2,128)} %eoff.3) | copy-start | bytes 12292
  0.7 76.0 %copy-start.11 = (f32[2,512]{1,0:T(2,128)S(1)}, f32[2,512]{1,0:T(2,128)}, u32[]{:S(2)}) copy-start(f32[2,512]{1,0:T(2,128)} %ngain.3) | copy-start | bytes 12292
  0.7 76.0 %copy-start.12 = (f32[2,512]{1,0:T(2,128)S(1)}, f32[2,512]{1,0:T(2,128)}, u32[]{:S(2)}) copy-start(f32[2,512]{1,0:T(2,128)} %noff.3) | copy-start | bytes 12292
  0.7 76.0 %copy-start.13 = (s32[20]{0:T(128)S(1)}, s32[20]{0:T(128)}, u32[]{:S(2)}) copy-start(s32[20]{0:T(128)} %counts.3) | copy-start | bytes 244
  76.8 2.5 %copy-start.1 = (f32[2560,512]{1,0:T(8,128)S(1)}, f32[2560,512]{1,0:T(8,128)}, u32[]{:S(2)}) copy-start(f32[2560,512]{1,0:T(8,128)} %get-tuple-element.9.pre) | copy-start | bytes 15728644
  79.2 1.1 %copy-start.4 = (f32[320,512]{1,0:T(8,128)S(1)}, f32[320,512]{1,0:T(8,128)}, u32[]{:S(2)}) copy-start(f32[320,512]{1,0:T(8,128)} %get-tuple-element.12.node) | copy-start | bytes 1966084
  80.3 1.1 %copy-start.5 = (f32[320,512]{1,0:T(8,128)S(1)}, f32[320,512]{1,0:T(8,128)}, u32[]{:S(2)}) copy-start(f32[320,512]{1,0:T(8,128)} %get-tuple-element.13.pv) | copy-start | bytes 1966084
  81.4 0.9 copy-start.6

commit v2 on v1

v2 whole, which is shorter than its diff:
```python
import functools

import jax
import jax.numpy as jnp
from jax import lax
from jax.experimental import pallas as pl
from jax.experimental.pallas import tpu as pltpu
from jax.sharding import PartitionSpec as P

MESH = pl.DeviceIdType.MESH
F32 = jnp.float32
BF16 = jnp.bfloat16
D = 512
HALF = 256
ROWS = 320
EDGE = 2560
BIG = 512
NBIG = EDGE // BIG
EPS = 1e-05


def dot(a, b):
    return jnp.dot(a, b, preferred_element_type=F32)


def swish(v):
    half = 0.5 * v
    return half + half * jnp.tanh(half)


def norm(v, gain, offset):
    centre = v - jnp.sum(v, axis=-1, keepdims=True) * (1.0 / D)
    spread = jnp.sum(centre * centre, axis=-1, keepdims=True) * (1.0 / D)
    return centre * lax.rsqrt(spread + EPS) * gain + offset


def column(row):
    return jnp.transpose(jnp.broadcast_to(row, (128, 128)))


def hot(match):
    return jnp.where(match, 1.0, 0.0).astype(BF16)


def lanes(base):
    return (lax.broadcasted_iota(jnp.int32, (128, 128), 1) + base).astype(F32)


def strip(i, size):
    return slice(i * size, (i + 1) * size)


def finish_edges(pre, state, hot_last, rows, counts, w2, gain, offset, hidden, low, done):
    for i in range(NBIG):
        r = strip(i, BIG)
        half = pre[r, :] + dot(hot_last[r, :], rows)
        hidden[r, :] = (half + half * jnp.tanh(half)).astype(BF16)
    row = lax.broadcasted_iota(jnp.int32, (128, 1), 0)
    for i in range(NBIG):
        r = strip(i, BIG)
        n = BIG // 128
        usable = jnp.concatenate([row < counts[i * n + j] for j in range(n)], axis=0)
        update = norm(dot(hidden[r, :], w2), gain, offset)
        value = state[r, :] + jnp.where(usable, update, 0.0)
        low[r, :] = value.astype(BF16)
        done(i, value)


def node_finish(pv, summed, v1, w2, gain, offset):
    hidden = swish(pv + dot(summed.astype(BF16), v1)).astype(BF16)
    return norm(dot(hidden, w2), gain, offset)


def place():
    p = lax.axis_index("patch")
    b = lax.axis_index("band")
    core = p % 2
    z = (p // 2) % 4
    x = ((p // 8) % 2) * 2 + b
    y = p // 16
    return p, b, core, x, y, z


def at(core, x, y, z):
    return ((y * 2 + x // 2) * 4 + z) * 2 + core, x % 2


def first_kernel(
    latents,
    edges,
    snd,
    rcv,
    counts,
    lists,
    we1,
    eb1,
    we2,
    egain,
    eoff,
    wn1,
    nb1,
    wn2,
    ngain,
    noff,
    pre,
    state,
    node,
    pv,
    last_rows,
    hot_last,
    hot_sum,
    w2_next,
    v1_next,
    v2_next,
    lat,
    hot_halo,
    hot_local,
    hot_send,
    w1,
    w2,
    v1,
    v2,
    band_out,
    band_in,
    low,
    hidden,
    edge_low,
    table,
    stage,
    recv,
    lat_sem,
    edge_sem,
    w_sem,
    band_send,
    band_recv,
    halo_send,
    halo_recv,
    greet,
):
    p, b, core, x, y, z = place()
    me = p * 2 + b
    barrier = pltpu.get_barrier_semaphore()
    plane = [(0, 0, dy, dz) for dy in range(4) for dz in range(4) if (dy, dz) != (0, 0)]
    line = [(dc, dx, 0, 0) for dc in range(2) for dx in range(4) if (dc, dx) != (0, 0)]

    def peer(dc, dx, dy, dz):
        return at((core + dc) % 2, (x + dx) % 4, (y + dy) % 4, (z + dz) % 4)

    lat_copy = pltpu.make_async_copy(latents, lat, lat_sem)
    lat_copy.start()
    for o in plane + line:
        pl.semaphore_signal(barrier, inc=1, device_id=peer(*o), device_id_type=MESH)

    for c in range(8):
        block = jnp.concatenate(
            [jnp.broadcast_to(lists[:, q : q + 1], (8, 128)) for q in range(16 * c, 16 * c + 16)], axis=0
        ).astype(F32)
        for t in range(3):
            wide = 128 if t < 2 else 64
            hot_send[strip(c, 128), t * 128 : t * 128 + wide] = hot(block == lanes(t * 128))[:, :wide]

    lat_copy.wait()
    edge_copies = [
        pltpu.make_async_copy(edges.at[pl.ds(i * BIG, BIG)], state.at[pl.ds(i * BIG, BIG)], edge_sem.at[i])
        for i in range(NBIG)
    ]
    w_copies = [
        pltpu.make_async_copy(we1, w1, w_sem.at[0]),
        pltpu.make_async_copy(wn1, v1, w_sem.at[1]),
        pltpu.make_async_copy(we2.at[0], w2, w_sem.at[2]),
        pltpu.make_async_copy(wn2.at[0], v2, w_sem.at[3]),
        pltpu.make_async_copy(we2.at[1], w2_next, w_sem.at[4]),
        pltpu.make_async_copy(wn1.at[1, pl.ds(D, D)], v1_next, w_sem.at[5]),
        pltpu.make_async_copy(wn2.at[1], v2_next, w_sem.at[6]),
    ]
    w_copies[0].start()
    for c in edge_copies:
        c.start()
    for c in w_copies[1:]:
        c.start()
    band_out[...] = lat[pl.ds((1 - b) * ROWS, ROWS), :].astype(BF16)

    pl.semaphore_wait(barrier, len(plane) + len(line))
    for o in line:
        pl.semaphore_signal(greet, inc=1, device_id=peer(*o), device_id_type=MESH)
    pl.semaphore_wait(greet, len(line))
    band_copy = pltpu.make_async_remote_copy(
        src_ref=band_out,
        dst_ref=band_in,
        send_sem=band_send,
        recv_sem=band_recv,
        device_id=(p, 1 - b),
        device_id_type=MESH,
    )
    band_copy.start()

    def hots(i, _):
        rows = pl.ds(pl.multiple_of(i * 128, 128), 128)
        s = column(snd[pl.ds(i, 1), :].astype(F32))
        r = column(rcv[pl.ds(i, 1), :].astype(F32)) + float(ROWS)
        lane = lax.broadcasted_iota(jnp.int32, (128, 128), 1)
        mixed = jnp.where(lane < 64, s, r)
        for t, source in enumerate((s, s, mixed, r, r)):
            hot_local[rows, t * 128 : t * 128 + 128] = hot(source == lanes(t * 128))
        for t in range(8):
            hot_halo[t // 2, rows, (t % 2) * 128 : (t % 2) * 128 + 128] = hot(s == lanes(ROWS + t * 128))
        target = jnp.where(lane[:1] < counts[i], rcv[pl.ds(i, 1), :], -1)
        hot_sum[:, rows] = hot(lax.broadcasted_iota(jnp.int32, (ROWS, 128), 0) == target)
        return 0

    lax.fori_loop(0, EDGE // 128, hots, 0)
    w_copies[0].wait()
    for i in range(NBIG):
        edge_copies[i].wait()
        r = strip(i, BIG)
        pre[r, :] = 0.5 * (dot(state[r, :].astype(BF16), w1[0, :D, :]) + eb1[0:1, :])

    band_copy.wait()
    own = lat[pl.ds(b * ROWS, ROWS), :]
    other = band_in[...].astype(F32)
    node[:, :HALF] = jnp.where(b == 0, own, other)
    node[:, HALF:] = jnp.where(b == 0, other, own)
    for c in w_copies[1:]:
        c.wait()

    ys = [(y + d) % 4 for d in range(4)]
    xs = [(x + d) % 4 for d in range(4)]

    def exchange(layer):
        low[...] = node[...].astype(BF16)
        table[:ROWS, :] = (0.5 * dot(low[...], w1[layer, D : 2 * D, :])).astype(BF16)
        for c in range(8):
            rows = dot(hot_send[strip(c, 128), :], table[:ROWS, :]).astype(BF16)
            stage[layer, c * 16 : c * 16 + 16] = rows.reshape(16, 8, D)
        recv[layer, me] = stage[layer, me]

        def send(k, px, bx):
            pltpu.make_async_remote_copy(
                src_ref=stage.at[layer, px * 2 + bx],
                dst_ref=recv.at[layer, me],
                send_sem=halo_send.at[layer],
                recv_sem=halo_recv.at[layer, k],
                device_id=(px, bx),
                device_id_type=MESH,
            ).start()

        for group in ((1, 3), (2,), (0,)):

            def some(m, _):
                near = ((z + m // 2) % 4) * 2 + (core + m % 2) % 2
                for dx in range(4):
                    for dy in group:
                        px = ys[dy] * 16 + (xs[dx] // 2) * 8 + near
                        if dx == 0 and dy == 0:
                            pl.when(m > 0)(functools.partial(send, dy, px, xs[dx] % 2))
                        else:
                            send(dy, px, xs[dx] % 2)
                return 0

            lax.fori_loop(0, 8, some, 0)
        table[ROWS:, :] = (0.5 * dot(low[...], w1[layer, 2 * D :, :])).astype(BF16)
        pv[...] = dot(low[...], v1[layer, :D, :]) + nb1[layer : layer + 1, :]

    def wait_plane(layer, dy):
        n = 31 if dy == 0 else 32
        pltpu.make_async_copy(
            stage.at[layer, pl.ds(0, n)], recv.at[layer, pl.ds(0, n)], halo_recv.at[layer, dy]
        ).wait()
        return (y + 4 - dy) % 4

    def plane_rows(layer, source):
        return recv[layer, pl.ds(source * 32, 32)].reshape(256, D)

    def halo_part(layer, dy):
        source = wait_plane(layer, dy)
        for i in range(NBIG):
            r = strip(i, BIG)
            pre[r, :] += dot(hot_halo[source, r, :], plane_rows(layer, source))

    def wait_sends(layer):
        pltpu.make_async_copy(
            stage.at[layer, pl.ds(0, 127)], recv.at[layer, pl.ds(0, 127)], halo_send.at[layer]
        ).wait()

    exchange(0)
    for i in range(NBIG):
        r = strip(i, BIG)
        pre[r, :] += dot(hot_local[r, :], table[...])
    for dy in (1, 3, 2):
        halo_part(0, dy)
    source = wait_plane(0, 0)

    def keep(i, value):
        state[strip(i, BIG), :] = value

    finish_edges(
        pre,
        state,
        hot_halo.at[source],
        plane_rows(0, source),
        counts,
        w2[...],
        egain[0:1, :],
        eoff[0:1, :],
        hidden,
        edge_low,
        keep,
    )
    total = dot(hot_sum[...], edge_low[...])
    node[...] += node_finish(pv[...], total, v1[0, D:, :], v2[...], ngain[0:1, :], noff[0:1, :])
    exchange(1)
    for i in range(NBIG):
        r = strip(i, BIG)
        pre[r, :] = 0.5 * (dot(edge_low[r, :], w1[1, :D, :]) + eb1[1:2, :]) + dot(hot_local[r, :], table[...])
    for dy in (1, 3, 2):
        halo_part(1, dy)
    wait_sends(0)
    hot_last[...] = hot_halo[y]
    last_rows[...] = plane_rows(1, wait_plane(1, 0))
    wait_sends(1)


def second_kernel(
    pre,
    state,
    node,
    pv,
    last_rows,
    hot_last,
    hot_sum,
    w2,
    v1,
    v2,
    counts,
    egain,
    eoff,
    ngain,
    noff,
    edge_out,
    node_out,
    result,
    hidden,
    low,
    out_sem,
):
    copies = []

    def put(i, value):
        result[strip(i, BIG), :] = value
        copies.append(
            pltpu.make_async_copy(
                result.at[pl.ds(i * BIG, BIG)], edge_out.at[pl.ds(i * BIG, BIG)], out_sem.at[i]
            )
        )
        copies[-1].start()

    finish_edges(
        pre,
        state,
        hot_last,
        last_rows[...],
        counts,
        w2[...],
        egain[1:2, :],
        eoff[1:2, :],
        hidden,
        low,
        put,
    )
    total = dot(hot_sum[...], low[...])
    node_out[...] = node[...] + node_finish(pv[...], total, v1[...], v2[...], ngain[1:2, :], noff[1:2, :])
    for c in copies:
        c.wait()


VMEM = pl.BlockSpec(memory_space=pltpu.VMEM)
SMEM = pl.BlockSpec(memory_space=pltpu.SMEM)
ANY = pl.BlockSpec(memory_space=pl.ANY)
HBM = pl.BlockSpec(memory_space=pltpu.HBM)


def shards(
    latents,
    edge_latents,
    edge_sender,
    edge_receiver,
    block_counts,
    send_rows,
    edge_first_weight,
    edge_first_bias,
    edge_second_weight,
    edge_gain,
    edge_offset,
    node_first_weight,
    node_first_bias,
    node_second_weight,
    node_gain,
    node_offset,
):
    snd = edge_sender.reshape(EDGE // 128, 128)
    rcv = edge_receiver.reshape(EDGE // 128, 128)
    lists = jnp.transpose(send_rows[0])
    shape = jax.ShapeDtypeStruct
    held = pl.pallas_call(
        first_kernel,
        out_shape=(
            pltpu.VMEM((EDGE, D), F32),
            pltpu.VMEM((EDGE, D), F32),
            pltpu.VMEM((ROWS, D), F32),
            pltpu.VMEM((ROWS, D), F32),
            pltpu.VMEM((256, D), BF16),
            pltpu.VMEM((EDGE, 256), BF16),
            pltpu.VMEM((ROWS, EDGE), BF16),
            pltpu.VMEM((D, D), BF16),
            pltpu.VMEM((D, D), BF16),
            pltpu.VMEM((D, D), BF16),
        ),
        in_specs=[HBM, HBM, VMEM, VMEM, SMEM, VMEM, HBM, VMEM, HBM, VMEM, VMEM, HBM, VMEM, HBM, VMEM, VMEM],
        out_specs=(VMEM,) * 10,
        scratch_shapes=[
            pltpu.VMEM((2 * ROWS, HALF), F32),
            pltpu.VMEM((4, EDGE, 256), BF16),
            pltpu.VMEM((EDGE, 2 * ROWS), BF16),
            pltpu.VMEM((1024, ROWS), BF16),
            pltpu.VMEM((2, 3 * D, D), BF16),
            pltpu.VMEM((D, D), BF16),
            pltpu.VMEM((2, 2 * D, D), BF16),
            pltpu.VMEM((D, D), BF16),
            pltpu.VMEM((ROWS, HALF), BF16),
            pltpu.VMEM((ROWS, HALF), BF16),
            pltpu.VMEM((ROWS, D), BF16),
            pltpu.VMEM((EDGE, D), BF16),
            pltpu.VMEM((EDGE, D), BF16),
            pltpu.VMEM((2 * ROWS, D), BF16),
            pltpu.VMEM((2, 128, 8, D), BF16),
            pltpu.VMEM((2, 128, 8, D), BF16),
            pltpu.SemaphoreType.DMA,
            pltpu.SemaphoreType.DMA((NBIG,)),
            pltpu.SemaphoreType.DMA((7,)),
            pltpu.SemaphoreType.DMA,
            pltpu.SemaphoreType.DMA,
            pltpu.SemaphoreType.DMA((2,)),
            pltpu.SemaphoreType.DMA((2, 4)),
            pltpu.SemaphoreType.REGULAR,
        ],
        compiler_params=pltpu.CompilerParams(
            collective_id=0, has_side_effects=True, vmem_limit_bytes=47 * 1024 * 1024
        ),
    )(
        latents,
        edge_latents,
        snd,
        rcv,
        block_counts,
        lists,
        edge_first_weight,
        edge_first_bias,
        edge_second_weight,
        edge_gain,
        edge_offset,
        node_first_weight,
        node_first_bias,
        node_second_weight,
        node_gain,
        node_offset,
    )
    new_edges, new_nodes = pl.pallas_call(
        second_kernel,
        out_shape=(shape((EDGE, D), F32), shape((ROWS, D), F32)),
        in_specs=[VMEM] * 10 + [SMEM] + [VMEM] * 4,
        out_specs=(ANY, VMEM),
        scratch_shapes=[
            pltpu.VMEM((EDGE, D), F32),
            pltpu.VMEM((EDGE, D), BF16),
            pltpu.VMEM((EDGE, D), BF16),
            pltpu.SemaphoreType.DMA((NBIG,)),
        ],
        compiler_params=pltpu.CompilerParams(vmem_limit_bytes=24 * 1024 * 1024),
    )(
        *held,
        block_counts,
        edge_gain,
        edge_offset,
        node_gain,
        node_offset,
    )
    return new_nodes, new_edges


def solution(mesh):
    split = P(("patch", "band"))
    return jax.shard_map(
        shards,
        mesh=mesh,
        in_specs=(
            P("patch", "band"),
            P(("patch", "band"), None),
            split,
            split,
            split,
            P(("patch", "band"), None, None),
        )
        + (P(),) * 10,
        out_specs=(P(("patch", "band"), None), P(("patch", "band"), None)),
        check_vma=False,
    )
```

time: 97.1 us -> 65 us (0.67)
  Pallas kernels: 90.1 us -> 63.8 us
  local copies, waits for them, and re-layouts: 5.64 us -> 0.02 us
    pallas_call x2, Pallas kernels: 90.1 us -> 63.8 us  [the longest x1 57.2 us: shards(): pl.pallas_call(first_kernel, out_shape=(pltpu.VMEM((EDGE, D), F32), pltpu...]
    unnamed x28 -> x10, local copies, waits for them, and re-layouts: 5.64 us -> 0.02 us
where the time goes in v2:
time: 65 us; the launch traced here: 64.7 us
  Pallas kernels  63.8 us (98%)
  between operations  0.88 us (1%)
    pallas_call x1, Pallas kernels, shards(): pl.pallas_call(first_kernel, out_shape=(pltpu.VMEM((EDGE, D), F32), pltpu...  57.2 us
    pallas_call x1, Pallas kernels, shards(): pl.pallas_call(second_kernel, out_shape=(shape((EDGE, D), F32), shape((RO...  6.63 us

profile of v2, /device:TPU:1, one launch (start us, length us, event | category | flops | bytes accessed | tf_op | source)
XLA Modules:
  0.0 64.7 jit_solution(16806469558542755382)
XLA Ops:
  0.6 0.0 copy-start
  0.6 0.0 copy-start.1
  0.7 0.0 copy-start.2
  0.7 0.0 copy-start.3
  0.7 0.0 copy-start.4
  0.7 57.2 %shard_map.167 = (f32[2560,512]{1,0:T(8,128)S(1)}, f32[2560,512]{1,0:T(8,128)S(1)}, f32[320,512]{1,0:T(8,128)S(1)}, f32[320,512]{1,0:T(8,128)S(1)}, bf16[256,512...) custom-call(f32[640,256]{1,0:T(8,128)} %latents.1, ...), custom_call_target="tpu_custom_call" | custom-call | tf_op jit(solution)/shard_map/pallas_call | solution.py:404
  57.9 0.0 copy-done
  57.9 0.0 copy-done.1
  57.9 0.0 copy-done.2
  57.9 0.0 copy-done.3
  57.9 0.0 copy-done.4
  58.0 6.6 %shard_map.168 = (f32[2560,512]{1,0:T(8,128)}, f32[320,512]{1,0:T(8,128)}) custom-call(f32[2560,512]{1,0:T(8,128)S(1)} %get-tuple-element.14.pre, f32[2560,512]{1,0:T(8,128)S(1)} %get-tuple-element.15.state, f32[320,512]{1,0:T(8,128)S(1)} %get-tuple-element.16.node, f32[320,512]{1,0:T(8,128)S(1)} %get-tuple-element.17.pv, ...), custom_call_target="tpu_custom_call" | custom-call | tf_op jit(solution)/shard_map/pallas_call | solution.py:467
Async XLA Ops:
  0.6 57.3 %copy-start = (f32[2,512]{1,0:T(2,128)S(1)}, f32[2,512]{1,0:T(2,128)}, u32[]{:S(2)}) copy-start(f32[2,512]{1,0:T(2,128)} %egain.3) | copy-start | bytes 12292
  0.6 57.3 %copy-start.1 = (f32[2,512]{1,0:T(2,128)S(1)}, f32[2,512]{1,0:T(2,128)}, u32[]{:S(2)}) copy-start(f32[2,512]{1,0:T(2,128)} %eoff.3) | copy-start | bytes 12292
  0.7 57.3 %copy-start.2 = (f32[2,512]{1,0:T(2,128)S(1)}, f32[2,512]{1,0:T(2,128)}, u32[]{:S(2)}) copy-start(f32[2,512]{1,0:T(2,128)} %ngain.3) | copy-start | bytes 12292
  0.7 57.3 %copy-start.3 = (f32[2,512]{1,0:T(2,128)S(1)}, f32[2,512]{1,0:T(2,128)}, u32[]{:S(2)}) copy-start(f32[2,512]{1,0:T(2,128)} %noff.3) | copy-start | bytes 12292
  0.7 57.3 %copy-start.4 = (s32[20]{0:T(128)S(1)}, s32[20]{0:T(128)}, u32[]{:S(2)}) copy-start(s32[20]{0:T(128)} %counts.3) | copy-start | bytes 244

commit v3 on v2

--- a/solution.py
+++ b/solution.py
@@ -88,20 +88,20 @@
 def first_kernel(
     latents,
     edges,
-    snd,
-    rcv,
-    counts,
-    lists,
+    snd_hbm,
+    rcv_hbm,
+    counts_hbm,
+    lists_hbm,
     we1,
-    eb1,
+    eb1_hbm,
     we2,
-    egain,
-    eoff,
+    egain_hbm,
+    eoff_hbm,
     wn1,
-    nb1,
+    nb1_hbm,
     wn2,
-    ngain,
-    noff,
+    ngain_hbm,
+    noff_hbm,
     pre,
     state,
     node,
@@ -112,6 +112,16 @@
     w2_next,
     v1_next,
     v2_next,
+    snd,
+    rcv,
+    counts,
+    lists,
+    eb1,
+    egain,
+    eoff,
+    nb1,
+    ngain,
+    noff,
     lat,
     hot_halo,
     hot_local,
@@ -128,6 +138,7 @@
     table,
     stage,
     recv,
+    list_sem,
     lat_sem,
     edge_sem,
     w_sem,
@@ -148,9 +159,39 @@
 
     lat_copy = pltpu.make_async_copy(latents, lat, lat_sem)
     lat_copy.start()
-    for o in plane + line:
+    list_copy = pltpu.make_async_copy(lists_hbm, lists, list_sem)
+    list_copy.start()
+    for o in line + plane:
         pl.semaphore_signal(barrier, inc=1, device_id=peer(*o), device_id_type=MESH)
-
+    w_copies = [
+        pltpu.make_async_copy(source, target, w_sem.at[i])
+        for i, (source, target) in enumerate(
+            (
+                (we1, w1),
+                (snd_hbm, snd),
+                (rcv_hbm, rcv),
+                (counts_hbm, counts),
+                (eb1_hbm, eb1),
+                (wn1, v1),
+                (nb1_hbm, nb1),
+                (we2.at[0], w2),
+                (egain_hbm, egain),
+                (eoff_hbm, eoff),
+                (wn2.at[0], v2),
+                (ngain_hbm, ngain),
+                (noff_hbm, noff),
+                (we2.at[1], w2_next),
+                (wn1.at[1, pl.ds(D, D)], v1_next),
+                (wn2.at[1], v2_next),
+            )
+        )
+    ]
+    edge_copies = [
+        pltpu.make_async_copy(edges.at[pl.ds(i * BIG, BIG)], state.at[pl.ds(i * BIG, BIG)], edge_sem.at[i])
+        for i in range(NBIG)
+    ]
+
+    list_copy.wait()
     for c in range(8):
         block = jnp.concatenate(
             [jnp.broadcast_to(lists[:, q : q + 1], (8, 128)) for q in range(16 * c, 16 * c + 16)], axis=0
@@ -160,30 +201,13 @@
             hot_send[strip(c, 128), t * 128 : t * 128 + wide] = hot(block == lanes(t * 128))[:, :wide]
 
     lat_copy.wait()
-    edge_copies = [
-        pltpu.make_async_copy(edges.at[pl.ds(i * BIG, BIG)], state.at[pl.ds(i * BIG, BIG)], edge_sem.at[i])
-        for i in range(NBIG)
-    ]
-    w_copies = [
-        pltpu.make_async_copy(we1, w1, w_sem.at[0]),
-        pltpu.make_async_copy(wn1, v1, w_sem.at[1]),
-        pltpu.make_async_copy(we2.at[0], w2, w_sem.at[2]),
-        pltpu.make_async_copy(wn2.at[0], v2, w_sem.at[3]),
-        pltpu.make_async_copy(we2.at[1], w2_next, w_sem.at[4]),
-        pltpu.make_async_copy(wn1.at[1, pl.ds(D, D)], v1_next, w_sem.at[5]),
-        pltpu.make_async_copy(wn2.at[1], v2_next, w_sem.at[6]),
-    ]
-    w_copies[0].start()
-    for c in edge_copies:
+    band_out[...] = lat[pl.ds((1 - b) * ROWS, ROWS), :].astype(BF16)
+    for c in w_copies[:5] + edge_copies + w_copies[5:]:
         c.start()
-    for c in w_copies[1:]:
-        c.start()
-    band_out[...] = lat[pl.ds((1 - b) * ROWS, ROWS), :].astype(BF16)
 
     pl.semaphore_wait(barrier, len(plane) + len(line))
     for o in line:
         pl.semaphore_signal(greet, inc=1, device_id=peer(*o), device_id_type=MESH)
-    pl.semaphore_wait(greet, len(line))
     band_copy = pltpu.make_async_remote_copy(
         src_ref=band_out,
         dst_ref=band_in,
@@ -193,6 +217,79 @@
         device_id_type=MESH,
     )
     band_copy.start()
+    w_copies[0].wait()
+    band_copy.wait()
+    own = lat[pl.ds(b * ROWS, ROWS), :]
+    other = band_in[...].astype(F32)
+    node[:, :HALF] = jnp.where(b == 0, own, other)
+    node[:, HALF:] = jnp.where(b == 0, other, own)
+
+    ys = [(y + d) % 4 for d in range(4)]
+    xs = [(x + d) % 4 for d in range(4)]
+
+    def exchange(layer):
+        low[...] = node[...].astype(BF16)
+        table[:ROWS, :] = (0.5 * dot(low[...], w1[layer, D : 2 * D, :])).astype(BF16)
+        for c in range(8):
+            rows = dot(hot_send[strip(c, 128), :], table[:ROWS, :]).astype(BF16)
+            stage[layer, c * 16 : c * 16 + 16] = rows.reshape(16, 8, D)
+        recv[layer, me] = stage[layer, me]
+        if layer == 0:
+            pl.semaphore_wait(greet, len(line))
+
+        def send(k, px, bx):
+            pltpu.make_async_remote_copy(
+                src_ref=stage.at[layer, px * 2 + bx],
+                dst_ref=recv.at[layer, me],
+                send_sem=halo_send.at[layer],
+                recv_sem=halo_recv.at[layer, k],
+                device_id=(px, bx),
+                device_id_type=MESH,
+            ).start()
+
+        for group in ((1, 3), (2,), (0,)):
+
+            def some(m, _):
+                near = ((z + m // 2) % 4) * 2 + (core + m % 2) % 2
+                for dx in range(4):
+                    for dy in group:
+                        px = ys[dy] * 16 + (xs[dx] // 2) * 8 + near
+                        if dx == 0 and dy == 0:
+                            pl.when(m > 0)(functools.partial(send, dy, px, xs[dx] % 2))
+                        else:
+                            send(dy, px, xs[dx] % 2)
+                return 0
+
+            lax.fori_loop(0, 8, some, 0)
+
+    def tables(layer):
+        table[ROWS:, :] = (0.5 * dot(low[...], w1[layer, 2 * D :, :])).astype(BF16)
+        pv[...] = dot(low[...], v1[layer, :D, :]) + nb1[layer : layer + 1, :]
+
+    def wait_plane(layer, dy):
+        n = 31 if dy == 0 else 32
+        pltpu.make_async_copy(
+            stage.at[layer, pl.ds(0, n)], recv.at[layer, pl.ds(0, n)], halo_recv.at[layer, dy]
+        ).wait()
+        return (y + 4 - dy) % 4
+
+    def plane_rows(layer, source):
+        return recv[layer, pl.ds(source * 32, 32)].reshape(256, D)
+
+    def halo_part(layer, dy):
+        source = wait_plane(layer, dy)
+        for i in range(NBIG):
+            r = strip(i, BIG)
+            pre[r, :] += dot(hot_halo[source, r, :], plane_rows(layer, source))
+
+    def wait_sends(layer):
+        pltpu.make_async_copy(
+            stage.at[layer, pl.ds(0, 127)], recv.at[layer, pl.ds(0, 127)], halo_send.at[layer]
+        ).wait()
+
+    exchange(0)
+    for c in w_copies[1:5]:
+        c.wait()
 
     def hots(i, _):
         rows = pl.ds(pl.multiple_of(i * 128, 128), 128)
@@ -209,86 +306,16 @@
         return 0
 
     lax.fori_loop(0, EDGE // 128, hots, 0)
-    w_copies[0].wait()
-    for i in range(NBIG):
-        edge_copies[i].wait()
-        r = strip(i, BIG)
-        pre[r, :] = 0.5 * (dot(state[r, :].astype(BF16), w1[0, :D, :]) + eb1[0:1, :])
-
-    band_copy.wait()
-    own = lat[pl.ds(b * ROWS, ROWS), :]
-    other = band_in[...].astype(F32)
-    node[:, :HALF] = jnp.where(b == 0, own, other)
-    node[:, HALF:] = jnp.where(b == 0, other, own)
-    for c in w_copies[1:]:
+    for c in edge_copies + w_copies[5:]:
         c.wait()
-
-    ys = [(y + d) % 4 for d in range(4)]
-    xs = [(x + d) % 4 for d in range(4)]
-
-    def exchange(layer):
-        low[...] = node[...].astype(BF16)
-        table[:ROWS, :] = (0.5 * dot(low[...], w1[layer, D : 2 * D, :])).astype(BF16)
-        for c in range(8):
-            rows = dot(hot_send[strip(c, 128), :], table[:ROWS, :]).astype(BF16)
-            stage[layer, c * 16 : c * 16 + 16] = rows.reshape(16, 8, D)
-        recv[layer, me] = stage[layer, me]
-
-        def send(k, px, bx):
-            pltpu.make_async_remote_copy(
-                src_ref=stage.at[layer, px * 2 + bx],
-                dst_ref=recv.at[layer, me],
-                send_sem=halo_send.at[layer],
-                recv_sem=halo_recv.at[layer, k],
-                device_id=(px, bx),
-                device_id_type=MESH,
-            ).start()
-
-        for group in ((1, 3), (2,), (0,)):
-
-            def some(m, _):
-                near = ((z + m // 2) % 4) * 2 + (core + m % 2) % 2
-                for dx in range(4):
-                    for dy in group:
-                        px = ys[dy] * 16 + (xs[dx] // 2) * 8 + near
-                        if dx == 0 and dy == 0:
-                            pl.when(m > 0)(functools.partial(send, dy, px, xs[dx] % 2))
-                        else:
-                            send(dy, px, xs[dx] % 2)
-                return 0
-
-            lax.fori_loop(0, 8, some, 0)
-        table[ROWS:, :] = (0.5 * dot(low[...], w1[layer, 2 * D :, :])).astype(BF16)
-        pv[...] = dot(low[...], v1[layer, :D, :]) + nb1[layer : layer + 1, :]
-
-    def wait_plane(layer, dy):
-        n = 31 if dy == 0 else 32
-        pltpu.make_async_copy(
-            stage.at[layer, pl.ds(0, n)], recv.at[layer, pl.ds(0, n)], halo_recv.at[layer, dy]
-        ).wait()
-        return (y + 4 - dy) % 4
-
-    def plane_rows(layer, source):
-        return recv[layer, pl.ds(source * 32, 32)].reshape(256, D)
-
-    def halo_part(layer, dy):
-        source = wait_plane(layer, dy)
-        for i in range(NBIG):
-            r = strip(i, BIG)
-            pre[r, :] += dot(hot_halo[source, r, :], plane_rows(layer, source))
-
-    def wait_sends(layer):
-        pltpu.make_async_copy(
-            stage.at[layer, pl.ds(0, 127)], recv.at[layer, pl.ds(0, 127)], halo_send.at[layer]
-        ).wait()
-
-    exchange(0)
+    tables(0)
     for i in range(NBIG):
         r = strip(i, BIG)
-        pre[r, :] += dot(hot_local[r, :], table[...])
-    for dy in (1, 3, 2):
+        edge_part = 0.5 * (dot(state[r, :].astype(BF16), w1[0, :D, :]) + eb1[0:1, :])
+        pre[r, :] = edge_part + dot(hot_local[r, :], table[...])
+    for dy in (0, 1, 3):
         halo_part(0, dy)
-    source = wait_plane(0, 0)
+    source = wait_plane(0, 2)
 
     def keep(i, value):
         state[strip(i, BIG), :] = value
@@ -309,14 +336,15 @@
     total = dot(hot_sum[...], edge_low[...])
     node[...] += node_finish(pv[...], total, v1[0, D:, :], v2[...], ngain[0:1, :], noff[0:1, :])
     exchange(1)
+    tables(1)
     for i in range(NBIG):
         r = strip(i, BIG)
         pre[r, :] = 0.5 * (dot(edge_low[r, :], w1[1, :D, :]) + eb1[1:2, :]) + dot(hot_local[r, :], table[...])
-    for dy in (1, 3, 2):
+    for dy in (0, 1, 3):
         halo_part(1, dy)
     wait_sends(0)
-    hot_last[...] = hot_halo[y]
-    last_rows[...] = plane_rows(1, wait_plane(1, 0))
+    hot_last[...] = hot_halo[(y + 2) % 4]
+    last_rows[...] = plane_rows(1, wait_plane(1, 2))
     wait_sends(1)
 
 
@@ -415,9 +443,16 @@
             pltpu.VMEM((D, D), BF16),
             pltpu.VMEM((D, D), BF16),
         ),
-        in_specs=[HBM, HBM, VMEM, VMEM, SMEM, VMEM, HBM, VMEM, HBM, VMEM, VMEM, HBM, VMEM, HBM, VMEM, VMEM],
+        in_specs=[HBM] * 16,
         out_specs=(VMEM,) * 10,
         scratch_shapes=[
+            pltpu.VMEM((EDGE // 128, 128), jnp.int32),
+            pltpu.VMEM((EDGE // 128, 128), jnp.int32),
+            pltpu.SMEM((EDGE // 128,), jnp.int32),
+            pltpu.VMEM((8, 128), jnp.int32),
+        ]
+        + [pltpu.VMEM((2, D), F32)] * 6
+        + [
             pltpu.VMEM((2 * ROWS, HALF), F32),
             pltpu.VMEM((4, EDGE, 256), BF16),
             pltpu.VMEM((EDGE, 2 * ROWS), BF16),
@@ -435,8 +470,9 @@
             pltpu.VMEM((2, 128, 8, D), BF16),
             pltpu.VMEM((2, 128, 8, D), BF16),
             pltpu.SemaphoreType.DMA,
+            pltpu.SemaphoreType.DMA,
             pltpu.SemaphoreType.DMA((NBIG,)),
-            pltpu.SemaphoreType.DMA((7,)),
+            pltpu.SemaphoreType.DMA((16,)),
             pltpu.SemaphoreType.DMA,
             pltpu.SemaphoreType.DMA,
             pltpu.SemaphoreType.DMA((2,)),

time: 65 us -> 62.9 us (0.968)
  Pallas kernels: 63.8 us -> 61.8 us
    pallas_call x1, Pallas kernels: 57.2 us -> 55.2 us  [shards(): pl.pallas_call(first_kernel, out_shape=(pltpu.VMEM((EDGE, D), F32), pltpu...]
where the time goes in v3:
time: 62.9 us; the launch traced here: 62.7 us
  Pallas kernels  61.8 us (98%)
  between operations  0.88 us (1%)
    pallas_call x1, Pallas kernels, shards(): pl.pallas_call(first_kernel, out_shape=(pltpu.VMEM((EDGE, D), F32), pltpu...  55.2 us
    pallas_call x1, Pallas kernels, shards(): pl.pallas_call(second_kernel, out_shape=(shape((EDGE, D), F32), shape((RO...  6.62 us

profile of v3, /device:TPU:1, one launch (start us, length us, event | category | flops | bytes accessed | tf_op | source)
XLA Modules:
  0.0 62.7 jit_solution(5993181940784565749)
XLA Ops:
  0.6 0.0 copy-start
  0.6 0.0 copy-start.1
  0.7 0.0 copy-start.2
  0.7 0.0 copy-start.3
  0.7 0.0 copy-start.4
  0.7 55.2 %shard_map.167 = (f32[2560,512]{1,0:T(8,128)S(1)}, f32[2560,512]{1,0:T(8,128)S(1)}, f32[320,512]{1,0:T(8,128)S(1)}, f32[320,512]{1,0:T(8,128)S(1)}, bf16[256,512...) custom-call(f32[640,256]{1,0:T(8,128)} %latents.1, ...), custom_call_target="tpu_custom_call" | custom-call | tf_op jit(solution)/shard_map/pallas_call | solution.py:432
  55.9 0.0 copy-done
  55.9 0.0 copy-done.1
  55.9 0.0 copy-done.2
  55.9 0.0 copy-done.3
  56.0 0.0 copy-done.4
  56.0 6.6 %shard_map.168 = (f32[2560,512]{1,0:T(8,128)}, f32[320,512]{1,0:T(8,128)}) custom-call(f32[2560,512]{1,0:T(8,128)S(1)} %get-tuple-element.14.pre, f32[2560,512]{1,0:T(8,128)S(1)} %get-tuple-element.15.state, f32[320,512]{1,0:T(8,128)S(1)} %get-tuple-element.16.node, f32[320,512]{1,0:T(8,128)S(1)} %get-tuple-element.17.pv, ...), custom_call_target="tpu_custom_call" | custom-call | tf_op jit(solution)/shard_map/pallas_call | solution.py:503
Async XLA Ops:
  0.6 55.3 %copy-start = (f32[2,512]{1,0:T(2,128)S(1)}, f32[2,512]{1,0:T(2,128)}, u32[]{:S(2)}) copy-start(f32[2,512]{1,0:T(2,128)} %egain.1) | copy-start | bytes 12292
  0.6 55.3 %copy-start.1 = (f32[2,512]{1,0:T(2,128)S(1)}, f32[2,512]{1,0:T(2,128)}, u32[]{:S(2)}) copy-start(f32[2,512]{1,0:T(2,128)} %eoff.1) | copy-start | bytes 12292
  0.7 55.3 %copy-start.2 = (f32[2,512]{1,0:T(2,128)S(1)}, f32[2,512]{1,0:T(2,128)}, u32[]{:S(2)}) copy-start(f32[2,512]{1,0:T(2,128)} %ngain.1) | copy-start | bytes 12292
  0.7 55.3 %copy-start.3 = (f32[2,512]{1,0:T(2,128)S(1)}, f32[2,512]{1,0:T(2,128)}, u32[]{:S(2)}) copy-start(f32[2,512]{1,0:T(2,128)} %noff.1) | copy-start | bytes 12292
  0.7 55.3 %copy-start.4 = (s32[20]{0:T(128)S(1)}, s32[20]{0:T(128)}, u32[]{:S(2)}) copy-start(s32[20]{0:T(128)} %counts.1) | copy-start | bytes 244

commit v4 on v3

--- a/solution.py
+++ b/solution.py
@@ -17,6 +17,7 @@
 BIG = 512
 NBIG = EDGE // BIG
 EPS = 1e-05
+ORDER = (1, 3, 2, 0)
 
 
 def dot(a, b):
@@ -230,12 +231,11 @@
     def exchange(layer):
         low[...] = node[...].astype(BF16)
         table[:ROWS, :] = (0.5 * dot(low[...], w1[layer, D : 2 * D, :])).astype(BF16)
-        for c in range(8):
-            rows = dot(hot_send[strip(c, 128), :], table[:ROWS, :]).astype(BF16)
-            stage[layer, c * 16 : c * 16 + 16] = rows.reshape(16, 8, D)
-        recv[layer, me] = stage[layer, me]
-        if layer == 0:
-            pl.semaphore_wait(greet, len(line))
+
+        def fill(dy):
+            rows = pl.ds(pl.multiple_of(ys[dy] * 256, 256), 256)
+            chosen = dot(hot_send[rows, :], table[:ROWS, :]).astype(BF16)
+            stage[layer, pl.ds(ys[dy] * 32, 32)] = chosen.reshape(32, 8, D)
 
         def send(k, px, bx):
             pltpu.make_async_remote_copy(
@@ -247,20 +247,27 @@
                 device_id_type=MESH,
             ).start()
 
-        for group in ((1, 3), (2,), (0,)):
-
+        def send_plane(dy):
             def some(m, _):
                 near = ((z + m // 2) % 4) * 2 + (core + m % 2) % 2
                 for dx in range(4):
-                    for dy in group:
-                        px = ys[dy] * 16 + (xs[dx] // 2) * 8 + near
-                        if dx == 0 and dy == 0:
-                            pl.when(m > 0)(functools.partial(send, dy, px, xs[dx] % 2))
-                        else:
-                            send(dy, px, xs[dx] % 2)
+                    px = ys[dy] * 16 + (xs[dx] // 2) * 8 + near
+                    if dx == 0 and dy == 0:
+                        pl.when(m > 0)(functools.partial(send, dy, px, xs[dx] % 2))
+                    else:
+                        send(dy, px, xs[dx] % 2)
                 return 0
 
             lax.fori_loop(0, 8, some, 0)
+
+        fill(ORDER[0])
+        if layer == 0:
+            pl.semaphore_wait(greet, len(line))
+        for i in range(4):
+            if i < 3:
+                fill(ORDER[i + 1])
+            send_plane(ORDER[i])
+        recv[layer, me] = stage[layer, me]
 
     def tables(layer):
         table[ROWS:, :] = (0.5 * dot(low[...], w1[layer, 2 * D :, :])).astype(BF16)
@@ -313,9 +320,9 @@
         r = strip(i, BIG)
         edge_part = 0.5 * (dot(state[r, :].astype(BF16), w1[0, :D, :]) + eb1[0:1, :])
         pre[r, :] = edge_part + dot(hot_local[r, :], table[...])
-    for dy in (0, 1, 3):
+    for dy in ORDER[:3]:
         halo_part(0, dy)
-    source = wait_plane(0, 2)
+    source = wait_plane(0, ORDER[3])
 
     def keep(i, value):
         state[strip(i, BIG), :] = value
@@ -340,11 +347,11 @@
     for i in range(NBIG):
         r = strip(i, BIG)
         pre[r, :] = 0.5 * (dot(edge_low[r, :], w1[1, :D, :]) + eb1[1:2, :]) + dot(hot_local[r, :], table[...])
-    for dy in (0, 1, 3):
+    hot_last[...] = hot_halo[(y + 4 - ORDER[3]) % 4]
+    wait_sends(0)
+    for dy in ORDER[:3]:
         halo_part(1, dy)
-    wait_sends(0)
-    hot_last[...] = hot_halo[(y + 2) % 4]
-    last_rows[...] = plane_rows(1, wait_plane(1, 2))
+    last_rows[...] = plane_rows(1, wait_plane(1, ORDER[3]))
     wait_sends(1)
 
 

time: 62.9 us -> 60.2 us (0.957)
  Pallas kernels: 61.8 us -> 59.2 us
    pallas_call x1, Pallas kernels: 55.2 us -> 52.6 us  [shards(): pl.pallas_call(first_kernel, out_shape=(pltpu.VMEM((EDGE, D), F32), pltpu...]
where the time goes in v4:
time: 60.2 us; the launch traced here: 60.1 us
  Pallas kernels  59.2 us (98%)
  between operations  0.88 us (1%)
    pallas_call x1, Pallas kernels, shards(): pl.pallas_call(first_kernel, out_shape=(pltpu.VMEM((EDGE, D), F32), pltpu...  52.6 us
    pallas_call x1, Pallas kernels, shards(): pl.pallas_call(second_kernel, out_shape=(shape((EDGE, D), F32), shape((RO...  6.63 us

profile of v4, /device:TPU:1, one launch (start us, length us, event | category | flops | bytes accessed | tf_op | source)
XLA Modules:
  0.0 60.1 jit_solution(3322576656618344591)
XLA Ops:
  0.6 0.0 copy-start
  0.6 0.0 copy-start.1
  0.7 0.0 copy-start.2
  0.7 0.0 copy-start.3
  0.7 0.0 copy-start.4
  0.7 52.6 %shard_map.167 = (f32[2560,512]{1,0:T(8,128)S(1)}, f32[2560,512]{1,0:T(8,128)S(1)}, f32[320,512]{1,0:T(8,128)S(1)}, f32[320,512]{1,0:T(8,128)S(1)}, bf16[256,512...) custom-call(f32[640,256]{1,0:T(8,128)} %latents.1, ...), custom_call_target="tpu_custom_call" | custom-call | tf_op jit(solution)/shard_map/pallas_call | solution.py:439
  53.3 0.0 copy-done
  53.3 0.0 copy-done.1
  53.3 0.0 copy-done.2
  53.3 0.0 copy-done.3
  53.3 0.0 copy-done.4
  53.3 6.6 %shard_map.168 = (f32[2560,512]{1,0:T(8,128)}, f32[320,512]{1,0:T(8,128)}) custom-call(f32[2560,512]{1,0:T(8,128)S(1)} %get-tuple-element.14.pre, f32[2560,512]{1,0:T(8,128)S(1)} %get-tuple-element.15.state, f32[320,512]{1,0:T(8,128)S(1)} %get-tuple-element.16.node, f32[320,512]{1,0:T(8,128)S(1)} %get-tuple-element.17.pv, ...), custom_call_target="tpu_custom_call" | custom-call | tf_op jit(solution)/shard_map/pallas_call | solution.py:510
Async XLA Ops:
  0.6 52.6 %copy-start = (f32[2,512]{1,0:T(2,128)S(1)}, f32[2,512]{1,0:T(2,128)}, u32[]{:S(2)}) copy-start(f32[2,512]{1,0:T(2,128)} %egain.1) | copy-start | bytes 12292
  0.6 52.6 %copy-start.1 = (f32[2,512]{1,0:T(2,128)S(1)}, f32[2,512]{1,0:T(2,128)}, u32[]{:S(2)}) copy-start(f32[2,512]{1,0:T(2,128)} %eoff.1) | copy-start | bytes 12292
  0.7 52.6 %copy-start.2 = (f32[2,512]{1,0:T(2,128)S(1)}, f32[2,512]{1,0:T(2,128)}, u32[]{:S(2)}) copy-start(f32[2,512]{1,0:T(2,128)} %ngain.1) | copy-start | bytes 12292
  0.7 52.6 %copy-start.3 = (f32[2,512]{1,0:T(2,128)S(1)}, f32[2,512]{1,0:T(2,128)}, u32[]{:S(2)}) copy-start(f32[2,512]{1,0:T(2,128)} %noff.1) | copy-start | bytes 12292
  0.7 52.6 %copy-start.4 = (s32[20]{0:T(128)S(1)}, s32[20]{0:T(128)}, u32[]{:S(2)}) copy-start(s32[20]{0:T(128)} %counts.1) | copy-start | bytes 244

commit v5 on v3

--- a/solution.py
+++ b/solution.py
@@ -17,6 +17,8 @@
 BIG = 512
 NBIG = EDGE // BIG
 EPS = 1e-05
+STEP = 37
+UNSTEP = 45
 
 
 def dot(a, b):
@@ -83,6 +85,19 @@
 
 def at(core, x, y, z):
     return ((y * 2 + x // 2) * 4 + z) * 2 + core, x % 2
+
+
+def apart(step):
+    return step % 2, step // 2 % 4, step // 8 % 4, step // 32
+
+
+def together(dc, dx, dy, dz):
+    return dc % 2 + dx % 4 * 2 + dz % 4 * 8 + dy % 4 * 32
+
+
+def number(core, x, y, z):
+    patch, band = at(core % 2, x % 4, y % 4, z % 4)
+    return patch * 2 + band
 
 
 def first_kernel(
@@ -116,6 +131,7 @@
     rcv,
     counts,
     lists,
+    from_slot,
     eb1,
     egain,
     eoff,
@@ -191,15 +207,6 @@
         for i in range(NBIG)
     ]
 
-    list_copy.wait()
-    for c in range(8):
-        block = jnp.concatenate(
-            [jnp.broadcast_to(lists[:, q : q + 1], (8, 128)) for q in range(16 * c, 16 * c + 16)], axis=0
-        ).astype(F32)
-        for t in range(3):
-            wide = 128 if t < 2 else 64
-            hot_send[strip(c, 128), t * 128 : t * 128 + wide] = hot(block == lanes(t * 128))[:, :wide]
-
     lat_copy.wait()
     band_out[...] = lat[pl.ds((1 - b) * ROWS, ROWS), :].astype(BF16)
     for c in w_copies[:5] + edge_copies + w_copies[5:]:
@@ -217,6 +224,23 @@
         device_id_type=MESH,
     )
     band_copy.start()
+
+    list_copy.wait()
+    step = lax.broadcasted_iota(jnp.int32, (1, 128), 1) * STEP % 128
+    dc, dx, dz, dy = apart(step)
+    asks = (lax.broadcasted_iota(jnp.int32, (128, 128), 0) == number(core + dc, x + dx, y + dy, z + dz)).astype(F32)
+    asks = asks.astype(BF16)
+    high = lists[...] // 256
+    low_part = dot((lists[...] - 256 * high).astype(F32).astype(BF16), asks)
+    wanted = 256.0 * dot(high.astype(F32).astype(BF16), asks) + low_part
+    for c in range(8):
+        block = jnp.concatenate(
+            [jnp.broadcast_to(wanted[:, q : q + 1], (8, 128)) for q in range(16 * c, 16 * c + 16)], axis=0
+        )
+        for t in range(3):
+            wide = 128 if t < 2 else 64
+            hot_send[strip(c, 128), t * 128 : t * 128 + wide] = hot(block == lanes(t * 128))[:, :wide]
+
     w_copies[0].wait()
     band_copy.wait()
     own = lat[pl.ds(b * ROWS, ROWS), :]
@@ -224,63 +248,70 @@
     node[:, :HALF] = jnp.where(b == 0, own, other)
     node[:, HALF:] = jnp.where(b == 0, other, own)
 
-    ys = [(y + d) % 4 for d in range(4)]
     xs = [(x + d) % 4 for d in range(4)]
 
     def exchange(layer):
         low[...] = node[...].astype(BF16)
         table[:ROWS, :] = (0.5 * dot(low[...], w1[layer, D : 2 * D, :])).astype(BF16)
-        for c in range(8):
-            rows = dot(hot_send[strip(c, 128), :], table[:ROWS, :]).astype(BF16)
-            stage[layer, c * 16 : c * 16 + 16] = rows.reshape(16, 8, D)
-        recv[layer, me] = stage[layer, me]
+
+        def fill(c):
+            chosen = dot(hot_send[strip(c, 256), :], table[:ROWS, :]).astype(BF16)
+            stage[layer, strip(c, 32)] = chosen.reshape(32, 8, D)
+
+        def send_part(c):
+            def some(m, _):
+                for i in range(16):
+                    fixed = i * STEP % 128
+                    dc, dx = fixed % 2, fixed // 2 % 4
+                    turn = (m * (STEP * 16 % 128 // 16) + fixed // 16) % 8
+                    dz, dy = turn % 2 * 2 + fixed // 8 % 2, turn // 2
+                    px = (y + dy) % 4 * 16 + xs[dx] // 2 * 8 + (z + dz) % 4 * 2 + (core + dc) % 2
+
+                    def send():
+                        pltpu.make_async_remote_copy(
+                            src_ref=stage.at[layer, m * 16 + i],
+                            dst_ref=recv.at[layer, m * 16 + i],
+                            send_sem=halo_send.at[layer],
+                            recv_sem=halo_recv.at[layer, c],
+                            device_id=(px, xs[dx] % 2),
+                            device_id_type=MESH,
+                        ).start()
+
+                    if c == 0 and i == 0:
+                        pl.when(m > 0)(send)
+                    else:
+                        send()
+                return 0
+
+            lax.fori_loop(2 * c, 2 * c + 2, some, 0)
+
+        fill(0)
         if layer == 0:
             pl.semaphore_wait(greet, len(line))
-
-        def send(k, px, bx):
-            pltpu.make_async_remote_copy(
-                src_ref=stage.at[layer, px * 2 + bx],
-                dst_ref=recv.at[layer, me],
-                send_sem=halo_send.at[layer],
-                recv_sem=halo_recv.at[layer, k],
-                device_id=(px, bx),
-                device_id_type=MESH,
-            ).start()
-
-        for group in ((1, 3), (2,), (0,)):
-
-            def some(m, _):
-                near = ((z + m // 2) % 4) * 2 + (core + m % 2) % 2
-                for dx in range(4):
-                    for dy in group:
-                        px = ys[dy] * 16 + (xs[dx] // 2) * 8 + near
-                        if dx == 0 and dy == 0:
-                            pl.when(m > 0)(functools.partial(send, dy, px, xs[dx] % 2))
-                        else:
-                            send(dy, px, xs[dx] % 2)
-                return 0
-
-            lax.fori_loop(0, 8, some, 0)
+        for c in range(4):
+            if c < 3:
+                fill(c + 1)
+            send_part(c)
+        recv[layer, 0] = stage[layer, 0]
 
     def tables(layer):
         table[ROWS:, :] = (0.5 * dot(low[...], w1[layer, 2 * D :, :])).astype(BF16)
         pv[...] = dot(low[...], v1[layer, :D, :]) + nb1[layer : layer + 1, :]
 
-    def wait_plane(layer, dy):
-        n = 31 if dy == 0 else 32
+    def wait_part(layer, c):
+        n = 31 if c == 0 else 32
         pltpu.make_async_copy(
-            stage.at[layer, pl.ds(0, n)], recv.at[layer, pl.ds(0, n)], halo_recv.at[layer, dy]
+            stage.at[layer, pl.ds(0, n)], recv.at[layer, pl.ds(0, n)], halo_recv.at[layer, c]
         ).wait()
-        return (y + 4 - dy) % 4
-
-    def plane_rows(layer, source):
-        return recv[layer, pl.ds(source * 32, 32)].reshape(256, D)
-
-    def halo_part(layer, dy):
-        source = wait_plane(layer, dy)
+
+    def part_rows(layer, c):
+        return recv[layer, strip(c, 32)].reshape(256, D)
+
+    def halo_part(layer, c):
+        wait_part(layer, c)
         for i in range(NBIG):
             r = strip(i, BIG)
-            pre[r, :] += dot(hot_halo[source, r, :], plane_rows(layer, source))
+            pre[r, :] += dot(hot_halo[c, r, :], part_rows(layer, c))
 
     def wait_sends(layer):
         pltpu.make_async_copy(
@@ -291,16 +322,31 @@
     for c in w_copies[1:5]:
         c.wait()
 
+    remote = snd[...] - ROWS
+    dev = remote // 8
+    step = together(
+        core - dev // 2 % 2 + 2,
+        x - (dev // 16 % 2 * 2 + dev % 2) + 4,
+        y - dev // 32 + 4,
+        z - dev // 4 % 4 + 4,
+    )
+    place_of = ROWS + step * UNSTEP % 128 * 8 + remote % 8
+    from_slot[...] = jnp.where(remote < 0, snd[...], place_of).astype(F32)
+
     def hots(i, _):
         rows = pl.ds(pl.multiple_of(i * 128, 128), 128)
-        s = column(snd[pl.ds(i, 1), :].astype(F32))
+        s = column(from_slot[pl.ds(i, 1), :])
         r = column(rcv[pl.ds(i, 1), :].astype(F32)) + float(ROWS)
         lane = lax.broadcasted_iota(jnp.int32, (128, 128), 1)
         mixed = jnp.where(lane < 64, s, r)
         for t, source in enumerate((s, s, mixed, r, r)):
             hot_local[rows, t * 128 : t * 128 + 128] = hot(source == lanes(t * 128))
         for t in range(8):
-            hot_halo[t // 2, rows, (t % 2) * 128 : (t % 2) * 128 + 128] = hot(s == lanes(ROWS + t * 128))
+            part = hot(s == lanes(ROWS + t * 128))
+            if t < 6:
+                hot_halo[t // 2, rows, t % 2 * 128 : t % 2 * 128 + 128] = part
+            else:
+                hot_last[rows, t % 2 * 128 : t % 2 * 128 + 128] = part
         target = jnp.where(lane[:1] < counts[i], rcv[pl.ds(i, 1), :], -1)
         hot_sum[:, rows] = hot(lax.broadcasted_iota(jnp.int32, (ROWS, 128), 0) == target)
         return 0
@@ -313,9 +359,9 @@
         r = strip(i, BIG)
         edge_part = 0.5 * (dot(state[r, :].astype(BF16), w1[0, :D, :]) + eb1[0:1, :])
         pre[r, :] = edge_part + dot(hot_local[r, :], table[...])
-    for dy in (0, 1, 3):
-        halo_part(0, dy)
-    source = wait_plane(0, 2)
+    for c in range(3):
+        halo_part(0, c)
+    wait_part(0, 3)
 
     def keep(i, value):
         state[strip(i, BIG), :] = value
@@ -323,8 +369,8 @@
     finish_edges(
         pre,
         state,
-        hot_halo.at[source],
-        plane_rows(0, source),
+        hot_last,
+        part_rows(0, 3),
         counts,
         w2[...],
         egain[0:1, :],
@@ -340,11 +386,11 @@
     for i in range(NBIG):
         r = strip(i, BIG)
         pre[r, :] = 0.5 * (dot(edge_low[r, :], w1[1, :D, :]) + eb1[1:2, :]) + dot(hot_local[r, :], table[...])
-    for dy in (0, 1, 3):
-        halo_part(1, dy)
     wait_sends(0)
-    hot_last[...] = hot_halo[(y + 2) % 4]
-    last_rows[...] = plane_rows(1, wait_plane(1, 2))
+    for c in range(3):
+        halo_part(1, c)
+    wait_part(1, 3)
+    last_rows[...] = part_rows(1, 3)
     wait_sends(1)
 
 
@@ -450,11 +496,12 @@
             pltpu.VMEM((EDGE // 128, 128), jnp.int32),
             pltpu.SMEM((EDGE // 128,), jnp.int32),
             pltpu.VMEM((8, 128), jnp.int32),
+            pltpu.VMEM((EDGE // 128, 128), F32),
         ]
         + [pltpu.VMEM((2, D), F32)] * 6
         + [
             pltpu.VMEM((2 * ROWS, HALF), F32),
-            pltpu.VMEM((4, EDGE, 256), BF16),
+            pltpu.VMEM((3, EDGE, 256), BF16),
             pltpu.VMEM((EDGE, 2 * ROWS), BF16),
             pltpu.VMEM((1024, ROWS), BF16),
             pltpu.VMEM((2, 3 * D, D), BF16),

time: 62.9 us -> 57.7 us (0.917)
  Pallas kernels: 61.8 us -> 56.6 us
    pallas_call x1, Pallas kernels: 55.2 us -> 50 us  [shards(): pl.pallas_call(first_kernel, out_shape=(pltpu.VMEM((EDGE, D), F32), pltpu...]
where the time goes in v5:
time: 57.7 us; the launch traced here: 57.5 us
  Pallas kernels  56.6 us (98%)
  between operations  0.88 us (2%)
    pallas_call x1, Pallas kernels, shards(): pl.pallas_call(first_kernel, out_shape=(pltpu.VMEM((EDGE, D), F32), pltpu...  50 us
    pallas_call x1, Pallas kernels, shards(): pl.pallas_call(second_kernel, out_shape=(shape((EDGE, D), F32), shape((RO...  6.62 us

profile of v5, /device:TPU:1, one launch (start us, length us, event | category | flops | bytes accessed | tf_op | source)
XLA Modules:
  0.0 57.5 jit_solution(9011414059141266025)
XLA Ops:
  0.6 0.0 copy-start
  0.6 0.0 copy-start.1
  0.7 0.0 copy-start.2
  0.7 0.0 copy-start.3
  0.7 0.0 copy-start.4
  0.7 50.0 %shard_map.167 = (f32[2560,512]{1,0:T(8,128)S(1)}, f32[2560,512]{1,0:T(8,128)S(1)}, f32[320,512]{1,0:T(8,128)S(1)}, f32[320,512]{1,0:T(8,128)S(1)}, bf16[256,512...) custom-call(f32[640,256]{1,0:T(8,128)} %latents.1, ...), custom_call_target="tpu_custom_call" | custom-call | tf_op jit(solution)/shard_map/pallas_call | solution.py:478
  50.7 0.0 copy-done
  50.7 0.0 copy-done.1
  50.7 0.0 copy-done.2
  50.7 0.0 copy-done.3
  50.7 0.0 copy-done.4
  50.8 6.6 %shard_map.168 = (f32[2560,512]{1,0:T(8,128)}, f32[320,512]{1,0:T(8,128)}) custom-call(f32[2560,512]{1,0:T(8,128)S(1)} %get-tuple-element.14.pre, f32[2560,512]{1,0:T(8,128)S(1)} %get-tuple-element.15.state, f32[320,512]{1,0:T(8,128)S(1)} %get-tuple-element.16.node, f32[320,512]{1,0:T(8,128)S(1)} %get-tuple-element.17.pv, ...), custom_call_target="tpu_custom_call" | custom-call | tf_op jit(solution)/shard_map/pallas_call | solution.py:550
Async XLA Ops:
  0.6 50.1 %copy-start = (f32[2,512]{1,0:T(2,128)S(1)}, f32[2,512]{1,0:T(2,128)}, u32[]{:S(2)}) copy-start(f32[2,512]{1,0:T(2,128)} %egain.1) | copy-start | bytes 12292
  0.6 50.1 %copy-start.1 = (f32[2,512]{1,0:T(2,128)S(1)}, f32[2,512]{1,0:T(2,128)}, u32[]{:S(2)}) copy-start(f32[2,512]{1,0:T(2,128)} %eoff.1) | copy-start | bytes 12292
  0.7 50.1 %copy-start.2 = (f32[2,512]{1,0:T(2,128)S(1)}, f32[2,512]{1,0:T(2,128)}, u32[]{:S(2)}) copy-start(f32[2,512]{1,0:T(2,128)} %ngain.1) | copy-start | bytes 12292
  0.7 50.1 %copy-start.3 = (f32[2,512]{1,0:T(2,128)S(1)}, f32[2,512]{1,0:T(2,128)}, u32[]{:S(2)}) copy-start(f32[2,512]{1,0:T(2,128)} %noff.1) | copy-start | bytes 12292
  0.7 50.1 %copy-start.4 = (s32[20]{0:T(128)S(1)}, s32[20]{0:T(128)}, u32[]{:S(2)}) copy-start(s32[20]{0:T(128)} %counts.1) | copy-start | bytes 244

commit v6 on v5

--- a/solution.py
+++ b/solution.py
@@ -16,6 +16,8 @@
 EDGE = 2560
 BIG = 512
 NBIG = EDGE // BIG
+BLK = 256
+PART = 64
 EPS = 1e-05
 STEP = 37
 UNSTEP = 45
@@ -52,25 +54,40 @@
     return slice(i * size, (i + 1) * size)
 
 
-def finish_edges(pre, state, hot_last, rows, counts, w2, gain, offset, hidden, low, done):
+def usable_rows(counts, block):
+    row = lax.broadcasted_iota(jnp.int32, (128, 1), 0)
+    n = BIG // 128
+    return jnp.concatenate([row < counts[block * n + j] for j in range(n)], axis=0)
+
+
+def finish_edges(pre, state, hot_last, rows, counts, w2, gain, hidden, product, low, out, done):
     for i in range(NBIG):
         r = strip(i, BIG)
         half = pre[r, :] + dot(hot_last[r, :], rows)
         hidden[r, :] = (half + half * jnp.tanh(half)).astype(BF16)
-    row = lax.broadcasted_iota(jnp.int32, (128, 1), 0)
-    for i in range(NBIG):
-        r = strip(i, BIG)
-        n = BIG // 128
-        usable = jnp.concatenate([row < counts[i * n + j] for j in range(n)], axis=0)
-        update = norm(dot(hidden[r, :], w2), gain, offset)
-        value = state[r, :] + jnp.where(usable, update, 0.0)
-        low[r, :] = value.astype(BF16)
-        done(i, value)
-
-
-def node_finish(pv, summed, v1, w2, gain, offset):
-    hidden = swish(pv + dot(summed.astype(BF16), v1)).astype(BF16)
-    return norm(dot(hidden, w2), gain, offset)
+    row = lax.broadcasted_iota(jnp.int32, (PART, 1), 0)
+    for i in range(EDGE // BLK):
+        product[i % 2] = dot(hidden[strip(i, BLK), :], w2)
+        for j in range(BLK // PART):
+            first = i * BLK + j * PART
+            r = slice(first, first + PART)
+            value = product[i % 2, strip(j, PART), :]
+            centre = value - jnp.sum(value, axis=-1, keepdims=True) * (1.0 / D)
+            spread = jnp.sum(centre * centre, axis=-1, keepdims=True) * (1.0 / D)
+            scale = jnp.where(row + first % 128 < counts[first // 128], lax.rsqrt(spread + EPS), 0.0)
+            value = state[r, :] + centre * scale * gain
+            out[r, :] = value
+            low[r, :] = value.astype(BF16)
+        done(i)
+
+
+def finish_nodes(node, pv, total, v1, w2, gain, offset, done):
+    summed = total.astype(BF16)
+    parts = [strip(i, ROWS // 2) for i in range(2)]
+    hidden = [swish(pv[r, :] + dot(summed[r, :], v1)).astype(BF16) for r in parts]
+    results = [dot(h, w2) for h in hidden]
+    for i in range(2):
+        done(i, node[parts[i], :] + norm(results[i], gain, offset))
 
 
 def place():
@@ -150,6 +167,7 @@
     band_in,
     low,
     hidden,
+    product,
     edge_low,
     table,
     stage,
@@ -173,8 +191,12 @@
     def peer(dc, dx, dy, dz):
         return at((core + dc) % 2, (x + dx) % 4, (y + dy) % 4, (z + dz) % 4)
 
-    lat_copy = pltpu.make_async_copy(latents, lat, lat_sem)
-    lat_copy.start()
+    lat_copies = [
+        pltpu.make_async_copy(latents.at[pl.ds(d * ROWS, ROWS)], lat.at[pl.ds(d * ROWS, ROWS)], lat_sem.at[i])
+        for i, d in enumerate((1 - b, b))
+    ]
+    for c in lat_copies:
+        c.start()
     list_copy = pltpu.make_async_copy(lists_hbm, lists, list_sem)
     list_copy.start()
     for o in line + plane:
@@ -207,7 +229,7 @@
         for i in range(NBIG)
     ]
 
-    lat_copy.wait()
+    lat_copies[0].wait()
     band_out[...] = lat[pl.ds((1 - b) * ROWS, ROWS), :].astype(BF16)
     for c in w_copies[:5] + edge_copies + w_copies[5:]:
         c.start()
@@ -242,6 +264,7 @@
             hot_send[strip(c, 128), t * 128 : t * 128 + wide] = hot(block == lanes(t * 128))[:, :wide]
 
     w_copies[0].wait()
+    lat_copies[1].wait()
     band_copy.wait()
     own = lat[pl.ds(b * ROWS, ROWS), :]
     other = band_in[...].astype(F32)
@@ -359,12 +382,10 @@
         r = strip(i, BIG)
         edge_part = 0.5 * (dot(state[r, :].astype(BF16), w1[0, :D, :]) + eb1[0:1, :])
         pre[r, :] = edge_part + dot(hot_local[r, :], table[...])
+        state[r, :] += jnp.where(usable_rows(counts, i), eoff[0:1, :], 0.0)
     for c in range(3):
         halo_part(0, c)
     wait_part(0, 3)
-
-    def keep(i, value):
-        state[strip(i, BIG), :] = value
 
     finish_edges(
         pre,
@@ -374,18 +395,24 @@
         counts,
         w2[...],
         egain[0:1, :],
-        eoff[0:1, :],
         hidden,
+        product,
         edge_low,
-        keep,
+        state,
+        lambda i: None,
     )
+
+    def keep(i, value):
+        node[strip(i, ROWS // 2), :] = value
+
     total = dot(hot_sum[...], edge_low[...])
-    node[...] += node_finish(pv[...], total, v1[0, D:, :], v2[...], ngain[0:1, :], noff[0:1, :])
+    finish_nodes(node, pv, total, v1[0, D:, :], v2[...], ngain[0:1, :], noff[0:1, :], keep)
     exchange(1)
     tables(1)
     for i in range(NBIG):
         r = strip(i, BIG)
         pre[r, :] = 0.5 * (dot(edge_low[r, :], w1[1, :D, :]) + eb1[1:2, :]) + dot(hot_local[r, :], table[...])
+        state[r, :] += jnp.where(usable_rows(counts, i), eoff[1:2, :], 0.0)
     wait_sends(0)
     for c in range(3):
         halo_part(1, c)
@@ -407,25 +434,29 @@
     v2,
     counts,
     egain,
-    eoff,
     ngain,
     noff,
     edge_out,
     node_out,
     result,
+    nodes,
     hidden,
+    product,
     low,
-    out_sem,
+    edge_sem,
+    node_sem,
 ):
     copies = []
 
-    def put(i, value):
-        result[strip(i, BIG), :] = value
-        copies.append(
-            pltpu.make_async_copy(
-                result.at[pl.ds(i * BIG, BIG)], edge_out.at[pl.ds(i * BIG, BIG)], out_sem.at[i]
-            )
-        )
+    def put(i):
+        r = pl.ds(i * BLK, BLK)
+        copies.append(pltpu.make_async_copy(result.at[r], edge_out.at[r], edge_sem.at[i]))
+        copies[-1].start()
+
+    def put_nodes(i, value):
+        nodes[strip(i, ROWS // 2), :] = value
+        r = pl.ds(i * (ROWS // 2), ROWS // 2)
+        copies.append(pltpu.make_async_copy(nodes.at[r], node_out.at[r], node_sem.at[i]))
         copies[-1].start()
 
     finish_edges(
@@ -436,13 +467,14 @@
         counts,
         w2[...],
         egain[1:2, :],
-        eoff[1:2, :],
         hidden,
+        product,
         low,
+        result,
         put,
     )
     total = dot(hot_sum[...], low[...])
-    node_out[...] = node[...] + node_finish(pv[...], total, v1[...], v2[...], ngain[1:2, :], noff[1:2, :])
+    finish_nodes(node, pv, total, v1[...], v2[...], ngain[1:2, :], noff[1:2, :], put_nodes)
     for c in copies:
         c.wait()
 
@@ -512,12 +544,13 @@
             pltpu.VMEM((ROWS, HALF), BF16),
             pltpu.VMEM((ROWS, D), BF16),
             pltpu.VMEM((EDGE, D), BF16),
+            pltpu.VMEM((2, BLK, D), F32),
             pltpu.VMEM((EDGE, D), BF16),
             pltpu.VMEM((2 * ROWS, D), BF16),
             pltpu.VMEM((2, 128, 8, D), BF16),
             pltpu.VMEM((2, 128, 8, D), BF16),
             pltpu.SemaphoreType.DMA,
-            pltpu.SemaphoreType.DMA,
+            pltpu.SemaphoreType.DMA((2,)),
             pltpu.SemaphoreType.DMA((NBIG,)),
             pltpu.SemaphoreType.DMA((16,)),
             pltpu.SemaphoreType.DMA,
@@ -550,20 +583,22 @@
     new_edges, new_nodes = pl.pallas_call(
         second_kernel,
         out_shape=(shape((EDGE, D), F32), shape((ROWS, D), F32)),
-        in_specs=[VMEM] * 10 + [SMEM] + [VMEM] * 4,
-        out_specs=(ANY, VMEM),
+        in_specs=[VMEM] * 10 + [SMEM] + [VMEM] * 3,
+        out_specs=(ANY, ANY),
         scratch_shapes=[
             pltpu.VMEM((EDGE, D), F32),
+            pltpu.VMEM((ROWS, D), F32),
             pltpu.VMEM((EDGE, D), BF16),
+            pltpu.VMEM((2, BLK, D), F32),
             pltpu.VMEM((EDGE, D), BF16),
-            pltpu.SemaphoreType.DMA((NBIG,)),
+            pltpu.SemaphoreType.DMA((EDGE // BLK,)),
+            pltpu.SemaphoreType.DMA((2,)),
         ],
         compiler_params=pltpu.CompilerParams(vmem_limit_bytes=24 * 1024 * 1024),
     )(
         *held,
         block_counts,
         edge_gain,
-        edge_offset,
         node_gain,
         node_offset,
     )

time: 57.7 us -> 56.7 us (0.983)
  Pallas kernels: 56.6 us -> 55.7 us
    pallas_call x1, Pallas kernels: 6.62 us -> 5.88 us  [shards(): pl.pallas_call(second_kernel, out_shape=(shape((EDGE, D), F32), shape((RO...]
where the time goes in v6:
time: 56.7 us; the launch traced here: 56.5 us
  Pallas kernels  55.7 us (98%)
  between operations  0.87 us (2%)
    pallas_call x1, Pallas kernels, shards(): pl.pallas_call(first_kernel, out_shape=(pltpu.VMEM((EDGE, D), F32), pltpu...  49.8 us
    pallas_call x1, Pallas kernels, shards(): pl.pallas_call(second_kernel, out_shape=(shape((EDGE, D), F32), shape((RO...  5.88 us

profile of v6, /device:TPU:1, one launch (start us, length us, event | category | flops | bytes accessed | tf_op | source)
XLA Modules:
  0.0 56.5 jit_solution(11745950742926873420)
XLA Ops:
  0.6 0.0 copy-start
  0.6 0.0 copy-start.1
  0.7 0.0 copy-start.2
  0.7 0.0 copy-start.3
  0.7 49.8 %shard_map.167 = (f32[2560,512]{1,0:T(8,128)S(1)}, f32[2560,512]{1,0:T(8,128)S(1)}, f32[320,512]{1,0:T(8,128)S(1)}, f32[320,512]{1,0:T(8,128)S(1)}, bf16[256,512...) custom-call(f32[640,256]{1,0:T(8,128)} %latents.1, ...), custom_call_target="tpu_custom_call" | custom-call | tf_op jit(solution)/shard_map/pallas_call | solution.py:510
  50.5 0.0 copy-done
  50.5 0.0 copy-done.1
  50.5 0.0 copy-done.2
  50.5 0.0 copy-done.3
  50.5 5.9 %shard_map.168 = (f32[2560,512]{1,0:T(8,128)}, f32[320,512]{1,0:T(8,128)}) custom-call(f32[2560,512]{1,0:T(8,128)S(1)} %get-tuple-element.14.pre, f32[2560,512]{1,0:T(8,128)S(1)} %get-tuple-element.15.state, f32[320,512]{1,0:T(8,128)S(1)} %get-tuple-element.16.node, f32[320,512]{1,0:T(8,128)S(1)} %get-tuple-element.17.pv, ...), custom_call_target="tpu_custom_call" | custom-call | tf_op jit(solution)/shard_map/pallas_call | solution.py:583
Async XLA Ops:
  0.6 49.8 %copy-start = (f32[2,512]{1,0:T(2,128)S(1)}, f32[2,512]{1,0:T(2,128)}, u32[]{:S(2)}) copy-start(f32[2,512]{1,0:T(2,128)} %egain.1) | copy-start | bytes 12292
  0.6 49.8 %copy-start.1 = (f32[2,512]{1,0:T(2,128)S(1)}, f32[2,512]{1,0:T(2,128)}, u32[]{:S(2)}) copy-start(f32[2,512]{1,0:T(2,128)} %ngain.1) | copy-start | bytes 12292
  0.7 49.8 %copy-start.2 = (f32[2,512]{1,0:T(2,128)S(1)}, f32[2,512]{1,0:T(2,128)}, u32[]{:S(2)}) copy-start(f32[2,512]{1,0:T(2,128)} %noff.1) | copy-start | bytes 12292
  0.7 49.8 %copy-start.3 = (s32[20]{0:T(128)S(1)}, s32[20]{0:T(128)}, u32[]{:S(2)}) copy-start(s32[20]{0:T(128)} %counts.1) | copy-start | bytes 244

commit v7 on v6

--- a/solution.py
+++ b/solution.py
@@ -19,8 +19,8 @@
 BLK = 256
 PART = 64
 EPS = 1e-05
-STEP = 37
-UNSTEP = 45
+STEP = 59
+UNSTEP = 115
 
 
 def dot(a, b):
@@ -81,10 +81,10 @@
         done(i)
 
 
-def finish_nodes(node, pv, total, v1, w2, gain, offset, done):
-    summed = total.astype(BF16)
+def finish_nodes(node, pv, hot_sum, edge_low, v1, w2, gain, offset, done):
     parts = [strip(i, ROWS // 2) for i in range(2)]
-    hidden = [swish(pv[r, :] + dot(summed[r, :], v1)).astype(BF16) for r in parts]
+    sums = [dot(hot_sum[r, :], edge_low[...]).astype(BF16) for r in parts]
+    hidden = [swish(pv[r, :] + dot(v, v1)).astype(BF16) for r, v in zip(parts, sums)]
     results = [dot(h, w2) for h in hidden]
     for i in range(2):
         done(i, node[parts[i], :] + norm(results[i], gain, offset))
@@ -191,12 +191,12 @@
     def peer(dc, dx, dy, dz):
         return at((core + dc) % 2, (x + dx) % 4, (y + dy) % 4, (z + dz) % 4)
 
-    lat_copies = [
-        pltpu.make_async_copy(latents.at[pl.ds(d * ROWS, ROWS)], lat.at[pl.ds(d * ROWS, ROWS)], lat_sem.at[i])
-        for i, d in enumerate((1 - b, b))
-    ]
-    for c in lat_copies:
-        c.start()
+    half_rows = ROWS // 2
+    lat_copies = []
+    for i, d in enumerate((1 - b, 1 - b, b)):
+        r = pl.ds(d * ROWS + (i % 2) * half_rows, half_rows) if i < 2 else pl.ds(d * ROWS, ROWS)
+        lat_copies.append(pltpu.make_async_copy(latents.at[r], lat.at[r], lat_sem.at[i]))
+        lat_copies[-1].start()
     list_copy = pltpu.make_async_copy(lists_hbm, lists, list_sem)
     list_copy.start()
     for o in line + plane:
@@ -229,23 +229,28 @@
         for i in range(NBIG)
     ]
 
-    lat_copies[0].wait()
-    band_out[...] = lat[pl.ds((1 - b) * ROWS, ROWS), :].astype(BF16)
+    for i in range(2):
+        lat_copies[i].wait()
+        band_out[strip(i, half_rows), :] = lat[pl.ds((1 - b) * ROWS + i * half_rows, half_rows), :].astype(BF16)
     for c in w_copies[:5] + edge_copies + w_copies[5:]:
         c.start()
 
     pl.semaphore_wait(barrier, len(plane) + len(line))
     for o in line:
         pl.semaphore_signal(greet, inc=1, device_id=peer(*o), device_id_type=MESH)
-    band_copy = pltpu.make_async_remote_copy(
-        src_ref=band_out,
-        dst_ref=band_in,
-        send_sem=band_send,
-        recv_sem=band_recv,
-        device_id=(p, 1 - b),
-        device_id_type=MESH,
-    )
-    band_copy.start()
+    band_copies = []
+    for i in range(2):
+        r = pl.ds(i * half_rows, half_rows)
+        copy = pltpu.make_async_remote_copy(
+            src_ref=band_out.at[r],
+            dst_ref=band_in.at[r],
+            send_sem=band_send.at[i],
+            recv_sem=band_recv.at[i],
+            device_id=(p, 1 - b),
+            device_id_type=MESH,
+        )
+        copy.start()
+        band_copies.append(copy)
 
     list_copy.wait()
     step = lax.broadcasted_iota(jnp.int32, (1, 128), 1) * STEP % 128
@@ -263,58 +268,50 @@
             wide = 128 if t < 2 else 64
             hot_send[strip(c, 128), t * 128 : t * 128 + wide] = hot(block == lanes(t * 128))[:, :wide]
 
+    def project(layer, i):
+        r = strip(i, half_rows)
+        low[r, :] = node[r, :].astype(BF16)
+        table[r, :] = (0.5 * dot(low[r, :], w1[layer, D : 2 * D, :])).astype(BF16)
+
     w_copies[0].wait()
-    lat_copies[1].wait()
-    band_copy.wait()
-    own = lat[pl.ds(b * ROWS, ROWS), :]
-    other = band_in[...].astype(F32)
-    node[:, :HALF] = jnp.where(b == 0, own, other)
-    node[:, HALF:] = jnp.where(b == 0, other, own)
+    lat_copies[2].wait()
+    for i in range(2):
+        band_copies[i].wait()
+        r = strip(i, half_rows)
+        own = lat[pl.ds(b * ROWS + i * half_rows, half_rows), :]
+        other = band_in[r, :].astype(F32)
+        node[r, :HALF] = jnp.where(b == 0, own, other)
+        node[r, HALF:] = jnp.where(b == 0, other, own)
+        project(0, i)
 
     xs = [(x + d) % 4 for d in range(4)]
 
     def exchange(layer):
-        low[...] = node[...].astype(BF16)
-        table[:ROWS, :] = (0.5 * dot(low[...], w1[layer, D : 2 * D, :])).astype(BF16)
-
-        def fill(c):
-            chosen = dot(hot_send[strip(c, 256), :], table[:ROWS, :]).astype(BF16)
-            stage[layer, strip(c, 32)] = chosen.reshape(32, 8, D)
-
-        def send_part(c):
-            def some(m, _):
-                for i in range(16):
-                    fixed = i * STEP % 128
-                    dc, dx = fixed % 2, fixed // 2 % 4
-                    turn = (m * (STEP * 16 % 128 // 16) + fixed // 16) % 8
-                    dz, dy = turn % 2 * 2 + fixed // 8 % 2, turn // 2
-                    px = (y + dy) % 4 * 16 + xs[dx] // 2 * 8 + (z + dz) % 4 * 2 + (core + dc) % 2
-
-                    def send():
-                        pltpu.make_async_remote_copy(
-                            src_ref=stage.at[layer, m * 16 + i],
-                            dst_ref=recv.at[layer, m * 16 + i],
-                            send_sem=halo_send.at[layer],
-                            recv_sem=halo_recv.at[layer, c],
-                            device_id=(px, xs[dx] % 2),
-                            device_id_type=MESH,
-                        ).start()
-
-                    if c == 0 and i == 0:
-                        pl.when(m > 0)(send)
-                    else:
-                        send()
-                return 0
-
-            lax.fori_loop(2 * c, 2 * c + 2, some, 0)
-
-        fill(0)
+        def fill(first, last):
+            chosen = dot(hot_send[first * 8 : last * 8, :], table[:ROWS, :]).astype(BF16)
+            stage[layer, first:last] = chosen.reshape(last - first, 8, D)
+
+        def send(first, last):
+            for k in range(max(first, 1), last):
+                dc, dx, dz, dy = apart(k * STEP % 128)
+                px = (y + dy) % 4 * 16 + xs[dx] // 2 * 8 + (z + dz) % 4 * 2 + (core + dc) % 2
+                pltpu.make_async_remote_copy(
+                    src_ref=stage.at[layer, k],
+                    dst_ref=recv.at[layer, k],
+                    send_sem=halo_send.at[layer],
+                    recv_sem=halo_recv.at[layer, k // 32],
+                    device_id=(px, xs[dx] % 2),
+                    device_id_type=MESH,
+                ).start()
+
+        cuts = (0, 16, 32, 64, 96, 128)
+        fill(0, 16)
         if layer == 0:
             pl.semaphore_wait(greet, len(line))
-        for c in range(4):
-            if c < 3:
-                fill(c + 1)
-            send_part(c)
+        for i in range(1, 6):
+            if i < 5:
+                fill(cuts[i], cuts[i + 1])
+            send(cuts[i - 1], cuts[i])
         recv[layer, 0] = stage[layer, 0]
 
     def tables(layer):
@@ -404,9 +401,9 @@
 
     def keep(i, value):
         node[strip(i, ROWS // 2), :] = value
-
-    total = dot(hot_sum[...], edge_low[...])
-    finish_nodes(node, pv, total, v1[0, D:, :], v2[...], ngain[0:1, :], noff[0:1, :], keep)
+        project(1, i)
+
+    finish_nodes(node, pv, hot_sum, edge_low, v1[0, D:, :], v2[...], ngain[0:1, :], noff[0:1, :], keep)
     exchange(1)
     tables(1)
     for i in range(NBIG):
@@ -473,8 +470,7 @@
         result,
         put,
     )
-    total = dot(hot_sum[...], low[...])
-    finish_nodes(node, pv, total, v1[...], v2[...], ngain[1:2, :], noff[1:2, :], put_nodes)
+    finish_nodes(node, pv, hot_sum, low, v1[...], v2[...], ngain[1:2, :], noff[1:2, :], put_nodes)
     for c in copies:
         c.wait()
 
@@ -550,11 +546,11 @@
             pltpu.VMEM((2, 128, 8, D), BF16),
             pltpu.VMEM((2, 128, 8, D), BF16),
             pltpu.SemaphoreType.DMA,
-            pltpu.SemaphoreType.DMA((2,)),
+            pltpu.SemaphoreType.DMA((3,)),
             pltpu.SemaphoreType.DMA((NBIG,)),
             pltpu.SemaphoreType.DMA((16,)),
-            pltpu.SemaphoreType.DMA,
-            pltpu.SemaphoreType.DMA,
+            pltpu.SemaphoreType.DMA((2,)),
+            pltpu.SemaphoreType.DMA((2,)),
             pltpu.SemaphoreType.DMA((2,)),
             pltpu.SemaphoreType.DMA((2, 4)),
             pltpu.SemaphoreType.REGULAR,

time: 56.7 us -> 55.6 us (0.981)
  Pallas kernels: 55.7 us -> 54.5 us
    pallas_call x1, Pallas kernels: 49.8 us -> 48.7 us  [shards(): pl.pallas_call(first_kernel, out_shape=(pltpu.VMEM((EDGE, D), F32), pltpu...]
where the time goes in v7:
time: 55.6 us; the launch traced here: 55.4 us
  Pallas kernels  54.5 us (98%)
  between operations  0.89 us (2%)
    pallas_call x1, Pallas kernels, shards(): pl.pallas_call(first_kernel, out_shape=(pltpu.VMEM((EDGE, D), F32), pltpu...  48.7 us
    pallas_call x1, Pallas kernels, shards(): pl.pallas_call(second_kernel, out_shape=(shape((EDGE, D), F32), shape((RO...  5.82 us

profile of v7, /device:TPU:1, one launch (start us, length us, event | category | flops | bytes accessed | tf_op | source)
XLA Modules:
  0.0 55.4 jit_solution(1118068572135048749)
XLA Ops:
  0.6 0.0 copy-start
  0.6 0.0 copy-start.1
  0.7 0.0 copy-start.2
  0.7 0.0 copy-start.3
  0.7 48.7 %shard_map.167 = (f32[2560,512]{1,0:T(8,128)S(1)}, f32[2560,512]{1,0:T(8,128)S(1)}, f32[320,512]{1,0:T(8,128)S(1)}, f32[320,512]{1,0:T(8,128)S(1)}, bf16[256,512...) custom-call(f32[640,256]{1,0:T(8,128)} %latents.1, ...), custom_call_target="tpu_custom_call" | custom-call | tf_op jit(solution)/shard_map/pallas_call | solution.py:506
  49.4 0.0 copy-done
  49.4 0.0 copy-done.1
  49.4 0.0 copy-done.2
  49.4 0.0 copy-done.3
  49.4 5.8 %shard_map.168 = (f32[2560,512]{1,0:T(8,128)}, f32[320,512]{1,0:T(8,128)}) custom-call(f32[2560,512]{1,0:T(8,128)S(1)} %get-tuple-element.14.pre, f32[2560,512]{1,0:T(8,128)S(1)} %get-tuple-element.15.state, f32[320,512]{1,0:T(8,128)S(1)} %get-tuple-element.16.node, f32[320,512]{1,0:T(8,128)S(1)} %get-tuple-element.17.pv, ...), custom_call_target="tpu_custom_call" | custom-call | tf_op jit(solution)/shard_map/pallas_call | solution.py:579
Async XLA Ops:
  0.6 48.8 %copy-start = (f32[2,512]{1,0:T(2,128)S(1)}, f32[2,512]{1,0:T(2,128)}, u32[]{:S(2)}) copy-start(f32[2,512]{1,0:T(2,128)} %egain.1) | copy-start | bytes 12292
  0.6 48.8 %copy-start.1 = (f32[2,512]{1,0:T(2,128)S(1)}, f32[2,512]{1,0:T(2,128)}, u32[]{:S(2)}) copy-start(f32[2,512]{1,0:T(2,128)} %ngain.1) | copy-start | bytes 12292
  0.7 48.8 %copy-start.2 = (f32[2,512]{1,0:T(2,128)S(1)}, f32[2,512]{1,0:T(2,128)}, u32[]{:S(2)}) copy-start(f32[2,512]{1,0:T(2,128)} %noff.1) | copy-start | bytes 12292
  0.7 48.8 %copy-start.3 = (s32[20]{0:T(128)S(1)}, s32[20]{0:T(128)}, u32[]{:S(2)}) copy-start(s32[20]{0:T(128)} %counts.1) | copy-start | bytes 244

commit v8 on v7

--- a/solution.py
+++ b/solution.py
@@ -110,6 +110,10 @@
 
 def together(dc, dx, dy, dz):
     return dc % 2 + dx % 4 * 2 + dz % 4 * 8 + dy % 4 * 32
+
+
+def distance(k):
+    return sum(min(d, 4 - d) for d in apart(k * STEP % 128)[1:])
 
 
 def number(core, x, y, z):
@@ -292,7 +296,7 @@
             stage[layer, first:last] = chosen.reshape(last - first, 8, D)
 
         def send(first, last):
-            for k in range(max(first, 1), last):
+            for k in sorted(range(max(first, 1), last), key=lambda k: -distance(k)):
                 dc, dx, dz, dy = apart(k * STEP % 128)
                 px = (y + dy) % 4 * 16 + xs[dx] // 2 * 8 + (z + dz) % 4 * 2 + (core + dc) % 2
                 pltpu.make_async_remote_copy(

time: 55.6 us -> 54.9 us (0.987)
  Pallas kernels: 54.5 us -> 53.9 us
    pallas_call x1, Pallas kernels: 48.7 us -> 48.1 us  [shards(): pl.pallas_call(first_kernel, out_shape=(pltpu.VMEM((EDGE, D), F32), pltpu...]
where the time goes in v8:
time: 54.9 us; the launch traced here: 54.8 us
  Pallas kernels  53.9 us (98%)
  between operations  0.89 us (2%)
    pallas_call x1, Pallas kernels, shards(): pl.pallas_call(first_kernel, out_shape=(pltpu.VMEM((EDGE, D), F32), pltpu...  48.1 us
    pallas_call x1, Pallas kernels, shards(): pl.pallas_call(second_kernel, out_shape=(shape((EDGE, D), F32), shape((RO...  5.83 us

profile of v8, /device:TPU:1, one launch (start us, length us, event | category | flops | bytes accessed | tf_op | source)
XLA Modules:
  0.0 54.8 jit_solution(13382024026536587973)
XLA Ops:
  0.6 0.0 copy-start
  0.6 0.0 copy-start.1
  0.7 0.0 copy-start.2
  0.7 0.0 copy-start.3
  0.7 48.1 %shard_map.167 = (f32[2560,512]{1,0:T(8,128)S(1)}, f32[2560,512]{1,0:T(8,128)S(1)}, f32[320,512]{1,0:T(8,128)S(1)}, f32[320,512]{1,0:T(8,128)S(1)}, bf16[256,512...) custom-call(f32[640,256]{1,0:T(8,128)} %latents.1, ...), custom_call_target="tpu_custom_call" | custom-call | tf_op jit(solution)/shard_map/pallas_call | solution.py:510
  48.7 0.0 copy-done
  48.7 0.0 copy-done.1
  48.8 0.0 copy-done.2
  48.8 0.0 copy-done.3
  48.8 5.8 %shard_map.168 = (f32[2560,512]{1,0:T(8,128)}, f32[320,512]{1,0:T(8,128)}) custom-call(f32[2560,512]{1,0:T(8,128)S(1)} %get-tuple-element.14.pre, f32[2560,512]{1,0:T(8,128)S(1)} %get-tuple-element.15.state, f32[320,512]{1,0:T(8,128)S(1)} %get-tuple-element.16.node, f32[320,512]{1,0:T(8,128)S(1)} %get-tuple-element.17.pv, ...), custom_call_target="tpu_custom_call" | custom-call | tf_op jit(solution)/shard_map/pallas_call | solution.py:583
Async XLA Ops:
  0.6 48.1 %copy-start = (f32[2,512]{1,0:T(2,128)S(1)}, f32[2,512]{1,0:T(2,128)}, u32[]{:S(2)}) copy-start(f32[2,512]{1,0:T(2,128)} %egain.1) | copy-start | bytes 12292
  0.6 48.1 %copy-start.1 = (f32[2,512]{1,0:T(2,128)S(1)}, f32[2,512]{1,0:T(2,128)}, u32[]{:S(2)}) copy-start(f32[2,512]{1,0:T(2,128)} %ngain.1) | copy-start | bytes 12292
  0.7 48.1 %copy-start.2 = (f32[2,512]{1,0:T(2,128)S(1)}, f32[2,512]{1,0:T(2,128)}, u32[]{:S(2)}) copy-start(f32[2,512]{1,0:T(2,128)} %noff.1) | copy-start | bytes 12292
  0.7 48.1 %copy-start.3 = (s32[20]{0:T(128)S(1)}, s32[20]{0:T(128)}, u32[]{:S(2)}) copy-start(s32[20]{0:T(128)} %counts.1) | copy-start | bytes 244

commit v9 on v8

--- a/solution.py
+++ b/solution.py
@@ -17,7 +17,7 @@
 BIG = 512
 NBIG = EDGE // BIG
 BLK = 256
-PART = 64
+PART = 32
 EPS = 1e-05
 STEP = 59
 UNSTEP = 115

time: 54.9 us -> 54.9 us (level)
  no operation moved by 1% of the time
where the time goes in v9:
time: 54.9 us; the launch traced here: 54.8 us
  Pallas kernels  53.9 us (98%)
  between operations  0.89 us (2%)
    pallas_call x1, Pallas kernels, shards(): pl.pallas_call(first_kernel, out_shape=(pltpu.VMEM((EDGE, D), F32), pltpu...  48.1 us
    pallas_call x1, Pallas kernels, shards(): pl.pallas_call(second_kernel, out_shape=(shape((EDGE, D), F32), shape((RO...  5.82 us

profile of v9, /device:TPU:1, one launch (start us, length us, event | category | flops | bytes accessed | tf_op | source)
XLA Modules:
  0.0 54.8 jit_solution(1718819874984274672)
XLA Ops:
  0.6 0.0 copy-start
  0.6 0.0 copy-start.1
  0.7 0.0 copy-start.2
  0.7 0.0 copy-start.3
  0.7 48.1 %shard_map.167 = (f32[2560,512]{1,0:T(8,128)S(1)}, f32[2560,512]{1,0:T(8,128)S(1)}, f32[320,512]{1,0:T(8,128)S(1)}, f32[320,512]{1,0:T(8,128)S(1)}, bf16[256,512...) custom-call(f32[640,256]{1,0:T(8,128)} %latents.1, ...), custom_call_target="tpu_custom_call" | custom-call | tf_op jit(solution)/shard_map/pallas_call | solution.py:510
  48.8 0.0 copy-done
  48.8 0.0 copy-done.1
  48.8 0.0 copy-done.2
  48.8 0.0 copy-done.3
  48.8 5.8 %shard_map.168 = (f32[2560,512]{1,0:T(8,128)}, f32[320,512]{1,0:T(8,128)}) custom-call(f32[2560,512]{1,0:T(8,128)S(1)} %get-tuple-element.14.pre, f32[2560,512]{1,0:T(8,128)S(1)} %get-tuple-element.15.state, f32[320,512]{1,0:T(8,128)S(1)} %get-tuple-element.16.node, f32[320,512]{1,0:T(8,128)S(1)} %get-tuple-element.17.pv, ...), custom_call_target="tpu_custom_call" | custom-call | tf_op jit(solution)/shard_map/pallas_call | solution.py:583
Async XLA Ops:
  0.6 48.1 %copy-start = (f32[2,512]{1,0:T(2,128)S(1)}, f32[2,512]{1,0:T(2,128)}, u32[]{:S(2)}) copy-start(f32[2,512]{1,0:T(2,128)} %egain.1) | copy-start | bytes 12292
  0.6 48.1 %copy-start.1 = (f32[2,512]{1,0:T(2,128)S(1)}, f32[2,512]{1,0:T(2,128)}, u32[]{:S(2)}) copy-start(f32[2,512]{1,0:T(2,128)} %ngain.1) | copy-start | bytes 12292
  0.7 48.1 %copy-start.2 = (f32[2,512]{1,0:T(2,128)S(1)}, f32[2,512]{1,0:T(2,128)}, u32[]{:S(2)}) copy-start(f32[2,512]{1,0:T(2,128)} %noff.1) | copy-start | bytes 12292
  0.7 48.1 %copy-start.3 = (s32[20]{0:T(128)S(1)}, s32[20]{0:T(128)}, u32[]{:S(2)}) copy-start(s32[20]{0:T(128)} %counts.1) | copy-start | bytes 244
